TPU v7x, 32 devices: a whole 2x2x4 slice. The times are simulated.
32 devices in a mesh: gx: 4 (over z), gy: 4 (over y, x), gz: 2 (over core).
Axes of the slice: x: 2, y: 2, z: 4, core: 2. Of those that a mesh axis runs over, the one named last changes fastest.
Arguments:
- coarse_field: float32 [3, 128, 128, 512], P(None, 'gx', 'gy', 'gz'), may hold values from -6 to 6
- fine_field: float32 [3, 128, 16, 256], P(None, ('gx', 'gy', 'gz')), may hold values from -6 to 6
- viscosity: float32 [128, 16, 256], P(('gx', 'gy', 'gz')), may hold values from 0.1 to 1
- corners: int32 [64, 3], replicated, may hold values from 0 to 504, as said below
- grid_slot: int32 [64], replicated, may hold values from 0 to 127, as said below
- neighbors: int32 [64, 2], replicated, may hold values from -1 to 63, as said below
Outputs:
- fine_out: float32 [3, 128, 16, 256], P(None, ('gx', 'gy', 'gz'))
- coarse_out: float32 [3, 128, 128, 512], P(None, 'gx', 'gy', 'gz')
Inputs may be any that keep to these rules, and one draw needn't show every extreme that they name: Each box is 8 coarse cells on a side, its corner coordinates are multiples of 8, it lies inside the domain and inside one coarse brick of 32 x 32 x 256 cells, and different grids have different boxes. A brick holds either no box or exactly 4 boxes, which share their y and z corners and are grids of one wake. `grid_slot`: different grids have different slots. A grid's slot lies on a device with the same gz index as the brick that holds its box. Every device holds at most 4 grids, some device holds 4 grids in every draw, and all grids of one device lie in one brick. `neighbors`: entry 0 is the grid of the same wake whose box touches the grid's lower x face, entry 1 the one touching its upper x face, or -1 where there is none.
All inputs are finite; a program needn't handle non-finite values.
Results may differ from a plain program's by a relative error of at most 0.00005.
Values sent between devices are 32-bit elements; how exact they have to be, the bound alone decides.
A program may use at most 128 MiB of HBM per device.

v0:
```python
import jax
import jax.numpy as jnp
from jax import lax
from jax.sharding import PartitionSpec as P

B = 8
F = 16
SLOTS = 4
CUBE = 1024


step_rate = 0.15


def with_halo(cells, sides, width):
    for axis, dim in sides:
        count = lax.axis_size(axis)
        ends = count - 1
        head = lax.slice_in_dim(cells, 0, width, axis=dim)
        tail = lax.slice_in_dim(cells, cells.shape[dim] - width, cells.shape[dim], axis=dim)
        cells = jnp.concatenate(
            [
                lax.ppermute(tail, axis, [(i, (i + 1) % count) for i in range(ends)]),
                cells,
                lax.ppermute(head, axis, [((i + 1) % count, i) for i in range(ends)]),
            ],
            axis=dim,
        )
    return cells


def tables():
    side = B + 2
    fine_index = jnp.arange(F, dtype=jnp.int32)
    coarse_index = jnp.arange(side, dtype=jnp.int32)
    center = fine_index // 2 + 1
    other = jnp.where(fine_index % 2 == 0, center - 1, center + 1)
    tangent = 0.75 * (coarse_index[None, :] == center[:, None]).astype(jnp.float32) + 0.25 * (
        coarse_index[None, :] == other[:, None]
    ).astype(jnp.float32)
    low_side = 0.75 * (coarse_index == 0).astype(jnp.float32) + 0.25 * (coarse_index == 1).astype(
        jnp.float32
    )
    high_side = 0.75 * (coarse_index == side - 1).astype(jnp.float32) + 0.25 * (
        coarse_index == side - 2
    ).astype(jnp.float32)
    return (tangent, low_side, high_side)


def prolong_matrix():
    side = B + 2
    tangent, low_side, high_side = tables()
    blocks = [
        jnp.einsum("a,sb,tc->abcst", low_side, tangent, tangent),
        jnp.einsum("a,sb,tc->abcst", high_side, tangent, tangent),
        jnp.einsum("sa,b,tc->abcst", tangent, low_side, tangent),
        jnp.einsum("sa,b,tc->abcst", tangent, high_side, tangent),
        jnp.einsum("sa,tb,c->abcst", tangent, tangent, low_side),
        jnp.einsum("sa,tb,c->abcst", tangent, tangent, high_side),
    ]
    joined = jnp.concatenate([block.reshape(side**3, F * F) for block in blocks], axis=1)
    return jnp.pad(joined, ((0, CUBE - side**3), (0, 0)))


def advance(volume, visc_cells, ghost_faces, lower_plane, upper_plane):
    components = volume.shape[0]
    slots_here = volume.shape[1]
    cells_edge = volume.shape[2]
    plane_size = volume.shape[3]
    lane_ids = jnp.arange(plane_size, dtype=jnp.int32)
    lane_y = lane_ids // cells_edge
    lane_z = lane_ids % cells_edge
    x_minus = jnp.concatenate([lower_plane[:, :, None], volume[:, :, :-1]], axis=2)
    x_plus = jnp.concatenate([volume[:, :, 1:], upper_plane[:, :, None]], axis=2)
    shape_four = (components, slots_here, cells_edge, cells_edge)
    y_low = jnp.tile(ghost_faces[:, :, 2].reshape(shape_four), (1, 1, 1, cells_edge))
    y_high = jnp.tile(ghost_faces[:, :, 3].reshape(shape_four), (1, 1, 1, cells_edge))
    z_low = jnp.repeat(ghost_faces[:, :, 4].reshape(shape_four), cells_edge, axis=3)
    z_high = jnp.repeat(ghost_faces[:, :, 5].reshape(shape_four), cells_edge, axis=3)
    zero_row = jnp.zeros_like(volume[..., :cells_edge])
    zero_cell = jnp.zeros_like(volume[..., :1])
    y_minus = jnp.where(
        lane_y == 0, y_low, jnp.concatenate([zero_row, volume[..., :-cells_edge]], axis=-1)
    )
    y_plus = jnp.where(
        lane_y == cells_edge - 1,
        y_high,
        jnp.concatenate([volume[..., cells_edge:], zero_row], axis=-1),
    )
    z_minus = jnp.where(lane_z == 0, z_low, jnp.concatenate([zero_cell, volume[..., :-1]], axis=-1))
    z_plus = jnp.where(
        lane_z == cells_edge - 1, z_high, jnp.concatenate([volume[..., 1:], zero_cell], axis=-1)
    )
    neighbor_sum = x_minus + x_plus + y_minus + y_plus + z_minus + z_plus - 6.0 * volume
    return volume + step_rate * visc_cells[None] * neighbor_sum


def row_picker(needed):
    highest = lax.Precision.HIGHEST

    def collect_rows(total_count, piece, start):
        row_ids = jnp.arange(piece.shape[1], dtype=jnp.int32)
        select = (needed[:, None] == row_ids[None, :]).astype(jnp.float32)
        return jnp.einsum("sr,krw->ksw", select, piece, precision=highest)

    return collect_rows


def on_device(coarse_field, fine_field, viscosity, corners, grid_slot, neighbors):
    count_y = lax.axis_size("gy")
    count_z = lax.axis_size("gz")
    index_x = lax.axis_index("gx")
    index_y = lax.axis_index("gy")
    index_z = lax.axis_index("gz")
    brick_x = coarse_field.shape[1]
    brick_y = coarse_field.shape[2]
    brick_z = coarse_field.shape[3]
    grid_total = corners.shape[0]
    grid_ids = jnp.arange(grid_total, dtype=jnp.int32)
    my_device = (index_x * count_y + index_y) * count_z + index_z
    slot_range = jnp.arange(SLOTS, dtype=jnp.int32)
    highest = lax.Precision.HIGHEST
    home_x = corners[:, 0] // brick_x
    home_y = corners[:, 1] // brick_y
    home_z = corners[:, 2] // brick_z
    home_group = home_x * count_y + home_y
    in_brick = (home_x == index_x) & (home_y == index_y) & (home_z == index_z)
    box_x = (corners[:, 0] - home_x * brick_x) // B
    owner_group = grid_slot // SLOTS // count_z
    owner_local = grid_slot % SLOTS
    row_match = in_brick[None, :] & (box_x[None, :] == slot_range[:, None])
    row_present = jnp.any(row_match, axis=1)
    row_grid = jnp.sum(jnp.where(row_match, grid_ids[None, :], 0), axis=1)
    row_corner = corners[row_grid]
    local_y = row_corner[:, 1] - index_y * brick_y
    local_z = row_corner[:, 2] - index_z * brick_z
    anchor_y = jnp.max(jnp.where(row_present, local_y, 0))
    anchor_z = jnp.max(jnp.where(row_present, local_z, 0))
    zero_start = jnp.zeros((), jnp.int32)
    own_slots = my_device * SLOTS + slot_range
    own_match = grid_slot[None, :] == own_slots[:, None]
    slot_active = jnp.any(own_match, axis=1)
    slot_grid = jnp.sum(jnp.where(own_match, grid_ids[None, :], 0), axis=1)
    rimmed = with_halo(coarse_field, (("gx", 1), ("gy", 2), ("gz", 3)), 1)
    side = B + 2
    slab = lax.dynamic_slice(
        rimmed, (zero_start, zero_start, anchor_y, anchor_z), (3, brick_x + 2, side, side)
    )
    cube_list = [
        slab[:, index * B : index * B + side].reshape(3, side**3) for index in range(SLOTS)
    ]
    cubes = jnp.pad(jnp.stack(cube_list, axis=1), ((0, 0), (0, 0), (0, CUBE - side**3)))
    cubes = jnp.where(row_present[None, :, None], cubes, 0.0)
    weights = prolong_matrix()
    payload = jnp.dot(
        cubes.reshape(3 * SLOTS, CUBE),
        weights,
        precision=highest,
        preferred_element_type=jnp.float32,
    ).reshape(3, SLOTS, 6 * F * F)
    payload_width = payload.shape[-1]
    need_coarse = home_group[slot_grid] * SLOTS + box_x[slot_grid]
    empty_payload = jnp.zeros((3, SLOTS, payload_width), jnp.float32)
    picked = row_picker(need_coarse)(
        empty_payload, lax.all_gather(payload, ("gx", "gy"), axis=1, tiled=True), jnp.int32(0)
    )
    ghost_faces = picked.reshape(3, SLOTS, 6, F * F)
    slot_near = neighbors[slot_grid]
    low_grid = jnp.maximum(slot_near[:, 0], 0)
    high_grid = jnp.maximum(slot_near[:, 1], 0)
    low_row = owner_group[low_grid] * SLOTS + owner_local[low_grid]
    high_row = owner_group[high_grid] * SLOTS + owner_local[high_grid]
    my_planes = jnp.concatenate([fine_field[:, :, F - 1, :], fine_field[:, :, 0, :]], axis=-1)
    pick_low = row_picker(low_row)
    pick_high = row_picker(high_row)
    empty_plane = jnp.zeros((3, SLOTS, F * F), jnp.float32)
    piece = lax.all_gather(my_planes, ("gx", "gy"), axis=1, tiled=True)
    start = jnp.int32(0)
    from_low = pick_low(empty_plane, piece[..., : F * F], start)
    from_high = pick_high(empty_plane, piece[..., F * F :], start)
    has_low = slot_active & (slot_near[:, 0] >= 0)
    has_high = slot_active & (slot_near[:, 1] >= 0)
    lower_plane = jnp.where(has_low[None, :, None], from_low, ghost_faces[:, :, 0])
    upper_plane = jnp.where(has_high[None, :, None], from_high, ghost_faces[:, :, 1])
    advanced = advance(fine_field, viscosity, ghost_faces, lower_plane, upper_plane)
    fine_out = jnp.where(slot_active[None, :, None, None], advanced, 0.0)
    block_means = (
        advanced.reshape(3, SLOTS, B, 2, B, 2, B, 2).mean(axis=(3, 5, 7)).reshape(3, SLOTS, B**3)
    )
    need_average = owner_group[row_grid] * SLOTS + owner_local[row_grid]
    empty_means = jnp.zeros((3, SLOTS, B**3), jnp.float32)
    returned = row_picker(need_average)(
        empty_means, lax.all_gather(block_means, ("gx", "gy"), axis=1, tiled=True), jnp.int32(0)
    )
    start = (zero_start, zero_start, anchor_y, anchor_z)
    current = lax.dynamic_slice(coarse_field, start, (3, brick_x, B, B))
    new_block = returned.reshape(3, SLOTS * B, B, B)
    x_present = jnp.repeat(row_present, B)
    region = jnp.where(x_present[None, :, None, None], new_block, current)
    coarse_out = lax.dynamic_update_slice(coarse_field, region, start)
    return (fine_out, coarse_out)


def solution(mesh):
    in_specs = (
        P(None, "gx", "gy", "gz"),
        P(None, ("gx", "gy", "gz"), None, None),
        P(("gx", "gy", "gz"), None, None),
        P(),
        P(),
        P(),
    )
    out_specs = (P(None, ("gx", "gy", "gz"), None, None), P(None, "gx", "gy", "gz"))
    return jax.shard_map(
        on_device, mesh=mesh, in_specs=in_specs, out_specs=out_specs, check_vma=False
    )
```

profile of v0, /device:TPU:0, one launch (start us, length us, event | category | flops | bytes accessed | tf_op | source)
XLA Modules:
  0.0 374.8 jit_solution(13768544895804024597)
XLA Ops:
  7.3 1.9 copy.177
  9.2 1.7 copy-done
  11.5 5.6 %collective-permute-start = (f32[3,1,32,256]{3,2,1,0:T(8,128)}, f32[3,1,32,256]{3,2,1,0:T(8,128)}, u32[]{:S(2)}, u32[]{:S(2)}) collective-permute-start(f32[3,1,32,256]{3,2,1,0:T(8,128)} %get-tuple-element.23), channel_id=1, source_target_pairs={{0,8},{8,16},{16,24},{1,9},{9,17},{17,25},{2,10},{10,18},{18,26},{... | collective-permute-start | bytes 294920 | tf_op jit(solution)/shard_map/ppermute | solution.py:23
  17.1 1.3 collective-permute-start.1
  23.3 3.7 copy.119
  28.0 47.6 %all_gather.9 = f32[3,64,512]{2,0,1:T(4,128)} all-gather(f32[3,4,512]{2,0,1:T(4,128)S(1)} %pad_maximum_fusion.4), channel_id=1, replica_groups=mesh['gx'=4,'gy'=4,'gz'=2] {'gx','gy'}, dimensions={1}, use_global_device_ids=true | all-gather | bytes 417792 | tf_op jit(solution)/shard_map/all_gather | solution.py:177
  75.5 7.0 %multiply_bitcast_fusion.4 = (f32[10,10,10,16,16]{4,3,2,1,0:T(8,128)}, f32[10,10,10,16,16]{4,3,2,1,0:T(8,128)}) fusion(f32[16,10,10]{0,1,2:T(8,128)} %get-tuple-element.51, f32[16,10]{0,1:T(8,128)S(1)} %select_add_fusion, f32[16,10,10]{0,1,2:T(8,128)} %get-tuple-element.52), kind=kLoop, calls=%fused_computation.14 | loop fusion | flops 512000 | bytes 2061440 | tf_op jit(solution)/shard_map/a,sb,tc->abcst/transpose | solution.py:55
  82.6 6.8 %reshape.284 = f32[1000,256]{1,0:T(8,128)} reshape(f32[10,10,10,16,16]{4,3,2,1,0:T(8,128)} %get-tuple-element.49) | data formatting | bytes 2048000 | tf_op jit(solution)/shard_map/reshape | solution.py:61
  89.3 6.8 %reshape.283 = f32[1000,256]{1,0:T(8,128)} reshape(f32[10,10,10,16,16]{4,3,2,1,0:T(8,128)} %get-tuple-element.50) | data formatting | bytes 2048000 | tf_op jit(solution)/shard_map/reshape | solution.py:61
  96.1 2.3 constant_dynamic-update-slice_fusion.5
  98.5 12.6 %multiply_bitcast_fusion = (f32[10,10,10,16,16]{4,3,2,1,0:T(8,128)}, f32[10,10,10,16,16]{4,3,1,2,0:T(8,128)}, f32[10,10,10,16,16]{4,3,1,2,0:T(8,128)}, f32[10,10,10,16,16]{4,3,2,1,0:T(8,128)}) fusion(f32[10,16,10]{1,0,2:T(8,128)S(1)} %get-tuple-element.47, f32[16,10]{0,1:T(8,128)S(1)} %select_add_fusion, f32[10,16,10]{1,0,2:T(8,128)S(1)} %get-tuple-element.48), kind=kLoop, calls=%fused_computation.10 | loop fusion | flops 512000 | bytes 4109440 | tf_op jit(solution)/shard_map/sa,tb,c->abcst/transpose | solution.py:59
  111.1 6.8 %reshape.288 = f32[1000,256]{1,0:T(8,128)} reshape(f32[10,10,10,16,16]{4,3,2,1,0:T(8,128)} %get-tuple-element.41) | data formatting | bytes 2048000 | tf_op jit(solution)/shard_map/reshape | solution.py:61
  117.8 6.8 %reshape.287 = f32[1000,256]{1,0:T(8,128)} reshape(f32[10,10,10,16,16]{4,3,2,1,0:T(8,128)} %get-tuple-element.46) | data formatting | bytes 2048000 | tf_op jit(solution)/shard_map/reshape | solution.py:61
  124.6 7.6 %copy.134 = f32[10,10,10,16,16]{4,3,2,1,0:T(8,128)} copy(f32[10,10,10,16,16]{4,3,1,2,0:T(8,128)} %get-tuple-element.42) | data formatting | bytes 2048000 | tf_op jit(solution)/shard_map/sa,b,tc->abcst/transpose | solution.py:57
  132.2 6.8 %reshape.286 = f32[1000,256]{1,0:T(8,128)} reshape(f32[10,10,10,16,16]{4,3,2,1,0:T(8,128)} %copy.134) | data formatting | bytes 2048000 | tf_op jit(solution)/shard_map/reshape | solution.py:61
  139.0 7.6 %copy.133 = f32[10,10,10,16,16]{4,3,2,1,0:T(8,128)} copy(f32[10,10,10,16,16]{4,3,1,2,0:T(8,128)} %get-tuple-element.45) | data formatting | bytes 2048000 | tf_op jit(solution)/shard_map/sa,b,tc->abcst/transpose | solution.py:56
  146.5 6.8 %reshape.285 = f32[1000,256]{1,0:T(8,128)} reshape(f32[10,10,10,16,16]{4,3,2,1,0:T(8,128)} %copy.133) | data formatting | bytes 2048000 | tf_op jit(solution)/shard_map/reshape | solution.py:61
  154.4 2.5 constant_dynamic-update-slice_fusion.4
  156.9 2.3 constant_dynamic-update-slice_fusion.3
  159.2 2.3 constant_dynamic-update-slice_fusion.2
  161.5 1.1 constant_dynamic-update-slice_fusion.1
  162.6 1.1 constant_dynamic-update-slice_fusion
  164.6 1.0 copy.118
  165.6 1.0 copy.120
  166.6 1.3 collective-permute-start.2
  167.9 1.5 collective-permute-start.3
  170.3 4.4 %collective-permute-done.3 = f32[3,34,1,256]{3,1,2,0:T(8,128)S(1)} collective-permute-done((f32[3,34,1,256]{3,1,2,0:T(8,128)S(1)}, f32[3,34,1,256]{3,1,2,0:T(8,128)S(1)}, u32[]{:S(2)}, u32[]{:S(2)}) %collective-permute-start.3) | collective-permute-done | bytes 104480 | tf_op jit(solution)/shard_map/ppermute | solution.py:25
  175.4 2.6 fusion.59
  178.0 3.1 copy.122
  181.2 3.1 copy.121
  184.3 1.9 collective-permute-start.4
  186.2 1.3 collective-permute-start.5
  191.9 3.1 copy.124
  195.0 3.1 copy.123
  198.1 2.2 fusion.9
  201.3 6.8 %fusion = f32[3,4,1536]{2,0,1:T(4,128)} fusion(f32[1000,1536]{1,0:T(8,128)} %constant_dynamic-update-slice_fusion, f32[3,1,1000]{2,0,1:T(4,128)S(1)} %stack_reshape.15, f32[3,1,1000]{2,0,1:T(4,128)S(1)} %stack_reshape.14, f32[3,1,1000]{2,0,1:T(4,128)S(1)} %stack_reshape.13, f32[3,1,1000]{2,0,1:T(4,128)S(1)} %stack_reshape.12, pred[4]{0:T(512)(128)(4,1)} %copy-done.10), kind=kOutput, calls=%fused_computation.16 | convolution fusion | flops 226603008 | bytes 6265732 | tf_op jit(solution)/shard_map/dot_general | solution.py:155
  211.2 0.8 gather_fusion.2
  212.0 0.8 gather_fusion.1
  217.0 0.8 fusion.65
  217.9 46.6 %all-gather.2.cloned.1.call-done = f32[3,64,1536]{2,0,1:T(4,128)} async-done(((f32[3,4,1536]{2,0,1:T(4,128)}), f32[3,64,1536]{2,0,1:T(4,128)}) %all-gather.2.cloned.1.call-update) | async-done | bytes 1179664 | tf_op jit(solution)/shard_map/all_gather | solution.py:165
  264.6 2.2 convolution_bitcast_fusion
  272.3 0.9 tile.22
  273.2 2.0 broadcast_select_fusion
  275.2 4.0 %copy.143 = f32[3,4,16,256]{1,3,2,0:T(8,128)} copy(f32[3,4,16,256]{3,2,1,0:T(8,128)S(1)} %get-tuple-element.15) | data formatting | bytes 393216 | tf_op jit(solution)/shard_map/add | solution.py:95
  279.2 7.6 %reduce_sum.35 = f32[3,4,8,8,8]{1,4,3,2,0:T(8,128)S(1)} reduce(f32[3,4,8,2,8,2,8,2]{1,7,6,5,4,3,2,0:T(2,128)} %bitcast.114, f32[]{:T(128)} %constant.186.clone.1), dimensions={3,5,7}, to_apply=%region_6.7 | reduce | flops 43008 | bytes 221188 | tf_op jit(solution)/shard_map/reduce_sum | solution.py:188
  287.1 41.7 %all_gather.11 = f32[3,64,512]{2,0,1:T(4,128)S(1)} all-gather(f32[3,4,512]{2,0,1:T(4,128)S(1)} %copy.144), channel_id=1, replica_groups=mesh['gx'=4,'gy'=4,'gz'=2] {'gx','gy'}, dimensions={1}, use_global_device_ids=true | all-gather | bytes 417792 | tf_op jit(solution)/shard_map/all_gather | solution.py:193
  329.4 1.6 dynamic-slice_select_fusion
  331.0 36.5 %dynamic_update_slice.3 = f32[3,32,32,256]{3,2,1,0:T(8,128)} dynamic-update-slice(f32[3,32,32,256]{3,2,1,0:T(8,128)} %copy-done, f32[3,32,8,8]{3,2,1,0:T(8,128)S(1)} %dynamic-slice_select_fusion, s32[]{:T(128)} %constant.171.clone.1, s32[]{:T(128)} %constant.171.clone.1, s32[]{:T(128)S(6)} %select_n.236, s32[]{:T(128)S(6)} %select_n.237) | dynamic-update-slice | bytes 49156 | tf_op jit(solution)/shard_map/dynamic_update_slice | solution.py:200
  (138 shorter events, 22.9 us)
Async XLA Ops:
  7.2 20.7 %copy-start.1 = (f32[3,4,16,256]{3,2,1,0:T(8,128)S(1)}, f32[3,4,16,256]{3,2,1,0:T(8,128)}, u32[]{:S(2)}) copy-start(f32[3,4,16,256]{3,2,1,0:T(8,128)} %param.7) | copy-start | bytes 589828
  7.2 11.3 %copy-start.9 = (s32[64,3]{0,1:T(4,128)S(1)}, s32[64,3]{0,1:T(4,128)}, u32[]{:S(2)}) copy-start(s32[64,3]{0,1:T(4,128)} %param.9) | copy-start | bytes 2308
  7.2 11.3 %copy-start.20 = (s32[64]{0:T(128)S(1)}, s32[64]{0:T(128)}, u32[]{:S(2)}) copy-start(s32[64]{0:T(128)} %param.10) | copy-start | bytes 772
  7.2 12.5 %copy-start.15 = (s32[64,2]{0,1:T(2,128)S(1)}, s32[64,2]{0,1:T(2,128)}, u32[]{:S(2)}) copy-start(s32[64,2]{0,1:T(2,128)} %param.11) | copy-start | bytes 1540
  7.2 257.4 %all-gather.2.cloned.1.call-start = ((), (), s32[]{:S(2)}) async-start(), calls=%async_computation | async-start | bytes 1671168 | tf_op jit(solution)/shard_map/all_gather | solution.py:165
  9.2 1.7 copy-start
  11.5 153.1 %collective-permute-start = (f32[3,1,32,256]{3,2,1,0:T(8,128)}, f32[3,1,32,256]{3,2,1,0:T(8,128)}, u32[]{:S(2)}, u32[]{:S(2)}) collective-permute-start(f32[3,1,32,256]{3,2,1,0:T(8,128)} %get-tuple-element.23), channel_id=1, source_target_pairs={{0,8},{8,16},{16,24},{1,9},{9,17},{17,25},{2,10},{10,18},{18,26},{... | collective-permute-start | bytes 294920 | tf_op jit(solution)/shard_map/ppermute | solution.py:23
  17.1 148.5 %collective-permute-start.1 = (f32[3,1,32,256]{3,2,1,0:T(8,128)}, f32[3,1,32,256]{3,2,1,0:T(8,128)}, u32[]{:S(2)}, u32[]{:S(2)}) collective-permute-start(f32[3,1,32,256]{3,2,1,0:T(8,128)} %get-tuple-element.24), channel_id=1, source_target_pairs={{8,0},{16,8},{24,16},{9,1},{17,9},{25,17},{10,2},{18,10},{26,18},{... | collective-permute-start | bytes 294920 | tf_op jit(solution)/shard_map/ppermute | solution.py:25
  18.4 0.6 copy-start.22
  18.7 145.2 %copy-start.10 = (pred[4]{0:T(512)(128)(4,1)}, pred[4]{0:T(512)(128)(4,1)S(1)}, u32[]{:S(2)}) copy-start(pred[4]{0:T(512)(128)(4,1)S(1)} %fusion.48) | copy-start | bytes 16
  146.5 7.3 %copy-start.7 = (s32[64,3]{1,0:T(8,128)S(1)}, s32[64,3]{1,0:T(8,128)}, u32[]{:S(2)}) copy-start(s32[64,3]{1,0:T(8,128)} %copy.128) | copy-start | bytes 2308
  154.4 7.1 %copy-start.3 = (f32[1000,256]{1,0:T(8,128)S(1)}, f32[1000,256]{1,0:T(8,128)}, u32[]{:S(2)}) copy-start(f32[1000,256]{1,0:T(8,128)} %reshape.287) | copy-start | bytes 3072004
  154.4 8.2 %copy-start.2 = (f32[1000,256]{1,0:T(8,128)S(1)}, f32[1000,256]{1,0:T(8,128)}, u32[]{:S(2)}) copy-start(f32[1000,256]{1,0:T(8,128)} %reshape.288) | copy-start | bytes 3072004
  156.9 12.5 %copy-start.14 = (s32[4]{0:T(128)S(1)}, s32[4]{0:T(128)}, u32[]{:S(2)}) copy-start(s32[4]{0:T(128)} %get-tuple-element.7) | copy-start | bytes 52
  166.6 3.7 collective-permute-start.2
  167.9 6.8 %collective-permute-start.3 = (f32[3,34,1,256]{3,1,2,0:T(8,128)S(1)}, f32[3,34,1,256]{3,1,2,0:T(8,128)S(1)}, u32[]{:S(2)}, u32[]{:S(2)}) collective-permute-start(f32[3,34,1,256]{3,1,2,0:T(8,128)S(1)} %get-tuple-element.22), channel_id=1, source_target_pairs={{2,0},{4,2},{6,4},{3,1},{5,3},{7,5},{10,8},{12,10},{14,12},{11,9},... | collective-permute-start | bytes 313352 | tf_op jit(solution)/shard_map/ppermute | solution.py:25
  170.3 7.7 %copy-start.5 = (f32[3,34,1,256]{3,1,2,0:T(8,128)}, f32[3,34,1,256]{3,1,2,0:T(8,128)S(1)}, u32[]{:S(2)}) copy-start(f32[3,34,1,256]{3,1,2,0:T(8,128)S(1)} %collective-permute-done.2) | copy-start | bytes 313348
  174.7 3.3 copy-start.6
  184.3 10.7 %collective-permute-start.4 = (f32[3,34,34,1]{2,1,3,0:T(8,128)}, f32[3,34,34,1]{2,1,3,0:T(8,128)}, u32[]{:S(2)}, u32[]{:S(2)}) collective-permute-start(f32[3,34,34,1]{2,1,3,0:T(8,128)} %copy.121), channel_id=1, source_target_pairs={{0,1},{2,3},{4,5},{6,7},{8,9},{10,11},{12,13},{14,15},{16,17},{18,... | collective-permute-start | bytes 41624 | tf_op jit(solution)/shard_map/ppermute | solution.py:23
  186.2 5.7 %collective-permute-start.5 = (f32[3,34,34,1]{2,1,3,0:T(8,128)}, f32[3,34,34,1]{2,1,3,0:T(8,128)}, u32[]{:S(2)}, u32[]{:S(2)}) collective-permute-start(f32[3,34,34,1]{2,1,3,0:T(8,128)} %copy.122), channel_id=1, source_target_pairs={{1,0},{3,2},{5,4},{7,6},{9,8},{11,10},{13,12},{15,14},{17,16},{19,... | collective-permute-start | bytes 41624 | tf_op jit(solution)/shard_map/ppermute | solution.py:25
  200.5 13.5 %copy-start.11 = (pred[4]{0:T(512)(128)(4,1)S(1)}, pred[4]{0:T(512)(128)(4,1)}, u32[]{:S(2)}) copy-start(pred[4]{0:T(512)(128)(4,1)} %copy-done.10) | copy-start | bytes 16
  200.5 15.0 %copy-start.21 = (s32[64]{0:T(128)S(1)}, s32[64]{0:T(128)}, u32[]{:S(2)}) copy-start(s32[64]{0:T(128)} %param.10) | copy-start | bytes 772
  200.5 15.0 %copy-start.23 = (s32[4]{0:T(128)S(1)}, s32[4]{0:T(128)}, u32[]{:S(2)}) copy-start(s32[4]{0:T(128)} %copy-done.22) | copy-start | bytes 52
  200.5 15.7 %copy-start.12 = (pred[4]{0:T(512)(128)(4,1)S(1)}, pred[4]{0:T(512)(128)(4,1)}, u32[]{:S(2)}) copy-start(pred[4]{0:T(512)(128)(4,1)} %get-tuple-element.8) | copy-start | bytes 16
  200.5 15.7 %copy-start.13 = (pred[4]{0:T(512)(128)(4,1)S(1)}, pred[4]{0:T(512)(128)(4,1)}, u32[]{:S(2)}) copy-start(pred[4]{0:T(512)(128)(4,1)} %get-tuple-element.9) | copy-start | bytes 16
  200.5 15.7 %copy-start.8 = (f32[4,16,256]{2,1,0:T(8,128)S(1)}, f32[4,16,256]{2,1,0:T(8,128)}, u32[]{:S(2)}) copy-start(f32[4,16,256]{2,1,0:T(8,128)} %param.8) | copy-start | bytes 196612
  201.1 16.7 %copy-start.4 = (f32[3,64,512]{2,0,1:T(4,128)S(1)}, f32[3,64,512]{2,0,1:T(4,128)}, u32[]{:S(2)}) copy-start(f32[3,64,512]{2,0,1:T(4,128)} %all_gather.9) | copy-start | bytes 1179652
  201.3 63.3 %copy-start.16 = (s32[4]{0:T(128)S(1)}, s32[4]{0:T(128)}, u32[]{:S(2)}) copy-start(s32[4]{0:T(128)} %multiply_add_fusion.2) | copy-start | bytes 52
  269.5 3.7 copy-start.17
  269.5 3.7 copy-start.18
  279.2 49.6 %copy-start.19 = (s32[4]{0:T(128)S(1)}, s32[4]{0:T(128)}, u32[]{:S(2)}) copy-start(s32[4]{0:T(128)} %multiply_add_fusion) | copy-start | bytes 52
Sparse Core Ops, SparseCore 0:
  208.2 56.2 all-gather.1
where the time goes:
time: 379 us; the launch traced here: 375 us
  local copies, waits for them, and re-layouts  149 us (39%)
  blocking collectives  89.2 us (24%)
  waiting for transfers between devices  51.3 us (14%)
  other arithmetic  41.3 us (11%)
  between operations  21.4 us (6%)
  starting transfers between devices  12.9 us (3%)
  matrix products  9.71 us (3%)
    all_gather x1, blocking collectives, on_device(): piece = lax.all_gather(my_planes, ('gx', 'gy'), axis=1, tiled=True)  47.6 us
    all_gather x1, waiting for transfers between devices, on_device(): lax.all_gather(payload, ('gx', 'gy'), axis=1, tiled=True)  46.6 us
    all_gather x1, blocking collectives, on_device(): lax.all_gather(block_means, ('gx', 'gy'), axis=1, tiled=True)  41.7 us
    reshape x6, local copies, waits for them, and re-layouts, prolong_matrix(): block.reshape(side ** 3, F * F)  40.7 us
    dynamic_update_slice x1, local copies, waits for them, and re-layouts, on_device(): coarse_out = lax.dynamic_update_slice(coarse_field, region, start)  36.5 us
    unnamed x57, local copies, waits for them, and re-layouts  18.7 us
    transpose x1, other arithmetic, prolong_matrix(): jnp.einsum('sa,tb,c->abcst', tangent, tangent, high_side)  12.6 us
    ppermute x3, starting transfers between devices, with_halo(): lax.ppermute(tail, axis, [(i, (i + 1) % count) for i in range(ends)])  8.78 us
  transfers between devices with their start and end apart: 7, of which 3 were waited for; matrix products, arithmetic and copies ran while one was open for 30% of the time, Pallas kernels for 0%

commit v1 on v0

v1 whole, which is shorter than its diff:
```python
import functools
import numpy as np
import jax
import jax.numpy as jnp
from jax import lax
from jax.experimental import pallas as pl
from jax.experimental.pallas import tpu as pltpu
from jax.sharding import PartitionSpec as P

B = 8
F = 16
SLOTS = 4
SIDE = B + 2
LANES = 128
MEAN_ROWS = 16
step_rate = 0.15
HIGHEST = lax.Precision.HIGHEST


def up(n, m):
    return -(-n // m) * m


def tables():
    tangent = np.zeros((F, SIDE), np.float32)
    for f in range(F):
        c = f // 2 + 1
        tangent[f, c] = 0.75
        tangent[f, c - 1 if f % 2 == 0 else c + 1] = 0.25
    low = np.zeros((SIDE,), np.float32)
    low[0], low[1] = 0.75, 0.25
    return tangent, low, low[::-1].copy()


def ghost_matrix():
    tangent, low, high = tables()
    out = np.zeros((LANES, 2 * F * F), np.float32)
    edge = np.zeros((SIDE, SIDE, F, F), np.float32)
    edge[:, :, 0, :] += np.einsum("b,tc->bct", low, tangent)
    edge[:, :, F - 1, :] += np.einsum("b,tc->bct", high, tangent)
    edge[:, :, :, 0] += np.einsum("sb,c->bcs", tangent, low)
    edge[:, :, :, F - 1] += np.einsum("sb,c->bcs", tangent, high)
    out[: SIDE * SIDE, : F * F] = edge.reshape(SIDE * SIDE, F * F)
    out[: SIDE * SIDE, F * F :] = np.einsum("sb,tc->bcst", tangent, tangent).reshape(SIDE * SIDE, F * F)
    return out


def mean_matrices():
    lanes = np.zeros((F * F, LANES), np.float32)
    for y in range(F):
        for z in range(F):
            for half in range(2):
                lanes[y * F + z, half * 64 + (y // 2) * B + z // 2] = 0.125
    rows = np.zeros((2, SLOTS * MEAN_ROWS, 3 * SLOTS * F), np.float32)
    for half in range(2):
        for s in range(SLOTS):
            for k in range(3):
                for a in range(B // 2):
                    for p in range(2):
                        x = 2 * (half * (B // 2) + a) + p
                        rows[half, s * MEAN_ROWS + k * (B // 2) + a, (k * SLOTS + s) * F + x] = 1.0
    return lanes, rows


def dot(a, b):
    return jnp.dot(a, b, precision=HIGHEST, preferred_element_type=jnp.float32)


def fine_kernel(
    nx, ny, flags, slab, planes, fine, visc, kw, tmat, nmat, lane_mean, row_mean,
    fine_out, picked, slabs, plane_buf, mean_send, means, advs, send_sem, recv_sem, own_sem,
):
    count = nx * ny
    me = lax.axis_index("gx") * ny + lax.axis_index("gy")

    def peer(o):
        t = lax.rem(me + o, count)
        return {"gx": t // ny, "gy": lax.rem(t, ny)}

    def remote(o, which, src, dst):
        return pltpu.make_async_remote_copy(
            src_ref=src, dst_ref=dst, send_sem=send_sem.at[which, o], recv_sem=recv_sem.at[which, o],
            device_id=peer(o), device_id_type=pl.DeviceIdType.MESH,
        )

    def slab_copy(o):
        return remote(o, 0, slab, slabs.at[me])

    def plane_copy(o):
        return remote(o, 1, planes, plane_buf.at[pl.ds(me * SLOTS, SLOTS)])

    def mean_copy(o):
        return remote(o, 2, mean_send, means.at[pl.ds(me * SLOTS, SLOTS)])

    barrier = pltpu.get_barrier_semaphore()

    def greet(o, c):
        pl.semaphore_signal(barrier, inc=1, device_id=peer(o), device_id_type=pl.DeviceIdType.MESH)
        return c

    lax.fori_loop(1, count, greet, 0)
    own_slab = pltpu.make_async_copy(slab, slabs.at[me], own_sem.at[0])
    own_plane = pltpu.make_async_copy(planes, plane_buf.at[pl.ds(me * SLOTS, SLOTS)], own_sem.at[1])
    own_slab.start()
    own_plane.start()
    pl.semaphore_wait(barrier, count - 1)

    def send(o, c):
        slab_copy(o).start()
        plane_copy(o).start()
        return c

    lax.fori_loop(1, count, send, 0)
    own_slab.wait()
    own_plane.wait()

    def finish(o, c):
        slab_copy(o).wait()
        plane_copy(o).wait()
        return c

    lax.fori_loop(1, count, finish, 0)

    half = dot(slabs[flags[0]], kw[...])
    ghost = dot(tmat[...], half[:, : F * F])
    xface = dot(nmat[...], half[:, F * F :])
    lane = lax.broadcasted_iota(jnp.int32, (F, F * F), 1)
    row = lax.broadcasted_iota(jnp.int32, (F, F * F), 0)
    lz = lane % F
    for s in range(SLOTS):
        active = flags[1 + s] > 0
        low_near = plane_buf[flags[1 + SLOTS + s]]
        high_near = plane_buf[flags[1 + 2 * SLOTS + s]]
        has_low = flags[1 + 3 * SLOTS + s] > 0
        has_high = flags[1 + 4 * SLOTS + s] > 0
        for k in range(3):
            v = fine[k, s]
            r = (k * SLOTS + s) * 2
            lower = jnp.where(has_low, low_near[2 * k : 2 * k + 1], xface[r : r + 1])
            upper = jnp.where(has_high, high_near[2 * k + 1 : 2 * k + 2], xface[r + 1 : r + 2])
            total = jnp.where(row == 0, lower, pltpu.roll(v, 1, 0))
            total += jnp.where(row == F - 1, upper, pltpu.roll(v, F - 1, 0))
            total += jnp.where(lane < F, 0.0, pltpu.roll(v, F, 1))
            total += jnp.where(lane >= F * F - F, 0.0, pltpu.roll(v, F * F - F, 1))
            total += jnp.where(lz == 0, 0.0, pltpu.roll(v, 1, 1))
            total += jnp.where(lz == F - 1, 0.0, pltpu.roll(v, F * F - 1, 1))
            at = (k * SLOTS + s) * F
            total += ghost[at : at + F] - 6.0 * v
            adv = v + step_rate * visc[s] * total
            advs[at : at + F] = adv
            fine_out[k, s] = jnp.where(active, adv, 0.0)
    z = dot(advs[...], lane_mean[...])
    first = dot(row_mean[0], z)
    second = dot(row_mean[1], z)
    lane_m = lax.broadcasted_iota(jnp.int32, first.shape, 1)
    packed = jnp.where(lane_m < 64, first, second).reshape(SLOTS, MEAN_ROWS, LANES)
    mean_send[...] = packed
    for s in range(SLOTS):
        means[me * SLOTS + s] = packed[s]

    def send_mean(o, c):
        mean_copy(o).start()
        return c

    lax.fori_loop(1, count, send_mean, 0)

    def finish_mean(o, c):
        mean_copy(o).wait()
        return c

    lax.fori_loop(1, count, finish_mean, 0)
    for s in range(SLOTS):
        picked[s] = means[flags[1 + 5 * SLOTS + s]]


def coarse_kernel(at, field, rows, out):
    n = field.shape[0]
    out[...] = field[...]
    y = pl.multiple_of(at[0], B)
    z = at[1]
    r3 = lax.broadcast_in_dim(rows[...], (n, B, B * B), (0, 2))
    sub = lax.broadcasted_iota(jnp.int32, r3.shape, 1)
    ln = lax.broadcasted_iota(jnp.int32, r3.shape, 2)
    spread = jnp.where(ln // B == sub, r3, 0.0).reshape(n * B, B * B)
    width = field.shape[2]
    c_id = lax.broadcasted_iota(jnp.int32, (B * B, width), 0) % B
    z_id = lax.broadcasted_iota(jnp.int32, (B * B, width), 1)
    place = jnp.where(z_id == z + c_id, 1.0, 0.0)
    value = dot(spread, place).reshape(n, B, width)
    z3 = lax.broadcasted_iota(jnp.int32, value.shape, 2)
    inside = (z3 >= z) & (z3 < z + B) & (at[2] > 0)
    out[:, pl.ds(y, B), :] = jnp.where(inside, value, field[:, pl.ds(y, B), :])


def shift(low_part, high_part, axis):
    count = lax.axis_size(axis)
    low = lax.ppermute(high_part, axis, [(i, i + 1) for i in range(count - 1)])
    high = lax.ppermute(low_part, axis, [(i + 1, i) for i in range(count - 1)])
    return low, high


def cut_slab(field, y, z):
    nx, ny, nz = field.shape[1:]
    zlo, zhi = shift(field[..., :1], field[..., -1:], "gz")

    def wide(part, lo, hi):
        return jnp.concatenate([lo, part, hi], axis=3)

    first = wide(field[:, :1], zlo[:, :1], zhi[:, :1])
    last = wide(field[:, -1:], zlo[:, -1:], zhi[:, -1:])
    xlo, xhi = shift(first, last, "gx")

    def line(start, size):
        def cut(a):
            return lax.dynamic_slice_in_dim(a, start, size, axis=2)

        return jnp.concatenate([cut(xlo), wide(cut(field), cut(zlo), cut(zhi)), cut(xhi)], axis=1)

    ylo, yhi = shift(line(0, 1), line(ny - 1, 1), "gy")

    def zcut(a):
        return lax.dynamic_slice_in_dim(a, z, SIDE, axis=3)

    low = jnp.where(y == 0, zcut(ylo), zcut(line(jnp.maximum(y - 1, 0), 1)))
    high = jnp.where(y == ny - B, zcut(yhi), zcut(line(jnp.minimum(y + B, ny - 1), 1)))
    slab = jnp.concatenate([low, zcut(line(y, B)), high], axis=2)
    slab = slab.reshape(3 * (nx + 2), SIDE * SIDE)
    rows = up(3 * (nx + 2), 8)
    return jnp.pad(slab, ((0, rows - 3 * (nx + 2)), (0, LANES - SIDE * SIDE)))


def on_device(coarse_field, fine_field, viscosity, corners, grid_slot, neighbors):
    count_x = lax.axis_size("gx")
    count_y = lax.axis_size("gy")
    count_z = lax.axis_size("gz")
    count = count_x * count_y
    index_x = lax.axis_index("gx")
    index_y = lax.axis_index("gy")
    index_z = lax.axis_index("gz")
    brick_x, brick_y, brick_z = coarse_field.shape[1:]
    my_device = (index_x * count_y + index_y) * count_z + index_z
    slot_range = jnp.arange(SLOTS, dtype=jnp.int32)
    home_x = corners[:, 0] // brick_x
    home_y = corners[:, 1] // brick_y
    home_z = corners[:, 2] // brick_z
    in_brick = (home_x == index_x) & (home_y == index_y) & (home_z == index_z)
    box_x = (corners[:, 0] - home_x * brick_x) // B
    owner_row = grid_slot // (SLOTS * count_z) * SLOTS + grid_slot % SLOTS

    def pick(match, values):
        return jnp.sum(jnp.where(match, values[None, :], 0), axis=1)

    present = jnp.any(in_brick)
    anchor_y = jnp.max(jnp.where(in_brick, corners[:, 1] - index_y * brick_y, 0))
    anchor_z = jnp.max(jnp.where(in_brick, corners[:, 2] - index_z * brick_z, 0))
    row_match = in_brick[None, :] & (box_x[None, :] == slot_range[:, None])
    need_mean = pick(row_match, owner_row)
    own_match = grid_slot[None, :] == (my_device * SLOTS + slot_range)[:, None]
    active = jnp.any(own_match, axis=1)
    slot_box = pick(own_match, box_x)
    home = jnp.max(jnp.where(own_match, (home_x * count_y + home_y)[None, :], 0))
    near_low = pick(own_match, neighbors[:, 0])
    near_high = pick(own_match, neighbors[:, 1])
    has_low = active & (near_low >= 0)
    has_high = active & (near_high >= 0)
    grid_ids = jnp.arange(corners.shape[0], dtype=jnp.int32)
    low_row = pick(grid_ids[None, :] == near_low[:, None], owner_row)
    high_row = pick(grid_ids[None, :] == near_high[:, None], owner_row)
    flags = jnp.concatenate(
        [home[None], active.astype(jnp.int32), low_row, high_row,
         has_low.astype(jnp.int32), has_high.astype(jnp.int32), need_mean]
    ).astype(jnp.int32)

    slab = cut_slab(coarse_field, anchor_y, anchor_z)
    slab_rows = slab.shape[0]
    planes = jnp.stack([fine_field[:, :, F - 1, :], fine_field[:, :, 0, :]], axis=1)
    planes = planes.reshape(6, SLOTS, F * F).transpose(1, 0, 2)
    planes = jnp.pad(planes, ((0, 0), (0, 2), (0, 0)))

    k_id = jnp.arange(3, dtype=jnp.int32)[:, None, None, None]
    i_id = jnp.arange(F, dtype=jnp.int32)[None, None, :, None]
    r_id = jnp.arange(slab_rows, dtype=jnp.int32)[None, None, None, :]
    base = k_id * (brick_x + 2) + B * slot_box[None, :, None, None]
    center = i_id // 2 + 1
    other = jnp.where(i_id % 2 == 0, center - 1, center + 1)
    tmat = jnp.where(r_id == base + center, 0.75, jnp.where(r_id == base + other, 0.25, 0.0))
    tmat = tmat.reshape(3 * SLOTS * F, slab_rows).astype(jnp.float32)
    side_id = jnp.arange(2, dtype=jnp.int32)[None, None, :, None]
    outer = jnp.where(side_id == 0, 0, SIDE - 1)
    inner = jnp.where(side_id == 0, 1, SIDE - 2)
    nmat = jnp.where(r_id == base + outer, 0.75, jnp.where(r_id == base + inner, 0.25, 0.0))
    nmat = nmat.reshape(3 * SLOTS * 2, slab_rows).astype(jnp.float32)

    lane_mean, row_mean = mean_matrices()
    vmem = pl.BlockSpec(memory_space=pltpu.VMEM)
    fine_out, picked = pl.pallas_call(
        functools.partial(fine_kernel, count_x, count_y),
        out_shape=(
            jax.ShapeDtypeStruct(fine_field.shape, jnp.float32),
            jax.ShapeDtypeStruct((SLOTS, MEAN_ROWS, LANES), jnp.float32),
        ),
        in_specs=[pl.BlockSpec(memory_space=pltpu.SMEM)] + [vmem] * 9,
        out_specs=(vmem, vmem),
        scratch_shapes=[
            pltpu.VMEM((count, slab_rows, LANES), jnp.float32),
            pltpu.VMEM((count * SLOTS, 8, F * F), jnp.float32),
            pltpu.VMEM((SLOTS, MEAN_ROWS, LANES), jnp.float32),
            pltpu.VMEM((count * SLOTS, MEAN_ROWS, LANES), jnp.float32),
            pltpu.VMEM((3 * SLOTS * F, F * F), jnp.float32),
            pltpu.SemaphoreType.DMA((3, count)),
            pltpu.SemaphoreType.DMA((3, count)),
            pltpu.SemaphoreType.DMA((2,)),
        ],
        compiler_params=pltpu.CompilerParams(collective_id=0, has_side_effects=True),
        name="fine_step",
    )(
        flags, slab, planes, fine_field, viscosity, jnp.asarray(ghost_matrix()), tmat, nmat,
        jnp.asarray(lane_mean), jnp.asarray(row_mean),
    )
    rows = picked[:, : 3 * (B // 2)].reshape(SLOTS, 3, B // 2, 2, B * B)
    rows = rows.transpose(1, 0, 3, 2, 4).reshape(3 * brick_x, B * B)
    at = jnp.stack([anchor_y, anchor_z, present.astype(jnp.int32)]).astype(jnp.int32)
    block = 16
    coarse_out = pl.pallas_call(
        coarse_kernel,
        out_shape=jax.ShapeDtypeStruct((3 * brick_x, brick_y, brick_z), jnp.float32),
        grid_spec=pltpu.PrefetchScalarGridSpec(
            num_scalar_prefetch=1,
            grid=(3 * brick_x // block,),
            in_specs=[
                pl.BlockSpec((block, brick_y, brick_z), lambda i, at: (i, 0, 0)),
                pl.BlockSpec((block, B * B), lambda i, at: (i, 0)),
            ],
            out_specs=pl.BlockSpec((block, brick_y, brick_z), lambda i, at: (i, 0, 0)),
        ),
        name="coarse_fill",
    )(at, coarse_field.reshape(3 * brick_x, brick_y, brick_z), rows)
    return fine_out, coarse_out.reshape(coarse_field.shape)


def solution(mesh):
    in_specs = (
        P(None, "gx", "gy", "gz"),
        P(None, ("gx", "gy", "gz"), None, None),
        P(("gx", "gy", "gz"), None, None),
        P(),
        P(),
        P(),
    )
    out_specs = (P(None, ("gx", "gy", "gz"), None, None), P(None, "gx", "gy", "gz"))
    return jax.shard_map(
        on_device, mesh=mesh, in_specs=in_specs, out_specs=out_specs, check_vma=False
    )
```

time: 379 us -> 117 us (0.31)
  local copies, waits for them, and re-layouts: 149 us -> 16.8 us
  blocking collectives: 89.2 us -> 0 us
  Pallas kernels: 0 us -> 61.3 us
  waiting for transfers between devices: 51.3 us -> 6.32 us
  other arithmetic: 41.3 us -> 7.56 us
  between operations: 21.4 us -> 8.14 us
  matrix products: 9.71 us -> 0 us
    all_gather x2 -> x0, blocking collectives: 89.2 us -> none  [the longest x1 47.6 us: on_device(): piece = lax.all_gather(my_planes, ('gx', 'gy'), axis=1, tiled=True)]
    pallas_call x0 -> x2, Pallas kernels: none -> 61.3 us  [the longest x1 54.6 us: on_device(): pl.pallas_call(functools.partial(fine_kernel, count_x, count_y), out_shap...]
    all_gather x1 -> x0, waiting for transfers between devices: 46.6 us -> none  [on_device(): lax.all_gather(payload, ('gx', 'gy'), axis=1, tiled=True)]
    reshape x10 -> x3, local copies, waits for them, and re-layouts: 42.3 us -> 0.38 us  [the longest x1 0.27 us: cut_slab(): slab = slab.reshape(3 * (nx + 2), SIDE * SIDE)]
    dynamic_update_slice x1 -> x0, local copies, waits for them, and re-layouts: 36.5 us -> none  [on_device(): coarse_out = lax.dynamic_update_slice(coarse_field, region, start)]
    transpose x2 -> x0, other arithmetic: 19.6 us -> none  [the longest x1 12.6 us: prolong_matrix(): jnp.einsum('sa,tb,c->abcst', tangent, tangent, high_side)]
    unnamed x57 -> x15, local copies, waits for them, and re-layouts: 18.7 us -> 1.98 us
    transpose x2 -> x1, local copies, waits for them, and re-layouts: 15.1 us -> 0.63 us  [on_device(): rows = rows.transpose(1, 0, 3, 2, 4).reshape(3 * brick_x, B * B)]
  transfers between devices with their start and end apart: 7 -> 6, of which waited for: 3 -> 3; matrix products, arithmetic and copies ran while one was open for 30% -> 15% of each run, Pallas kernels for 0% -> 0%
where the time goes in v1:
time: 117 us
  Pallas kernels  61.3 us (52%)
  local copies, waits for them, and re-layouts  16.8 us (14%)
  starting transfers between devices  16.4 us (14%)
  between operations  8.14 us (7%)
  other arithmetic  7.56 us (6%)
  waiting for transfers between devices  6.32 us (5%)
    pallas_call x1, Pallas kernels, on_device(): pl.pallas_call(functools.partial(fine_kernel, count_x, count_y), out_shap...  54.6 us
    ppermute x3, starting transfers between devices, shift(): low = lax.ppermute(high_part, axis, [(i, i + 1) for i in range(count - 1)])  12.6 us
    pallas_call x1, Pallas kernels, on_device(): pl.pallas_call(coarse_kernel, out_shape=jax.ShapeDtypeStruct((3 * brick_x...  6.67 us
    ppermute x3, waiting for transfers between devices, shift(): high = lax.ppermute(low_part, axis, [(i + 1, i) for i in range(count - 1)])  5.77 us
    dynamic_slice x12, local copies, waits for them, and re-layouts, cut(): return lax.dynamic_slice_in_dim(a, start, size, axis=2)  5.4 us
    ppermute x3, starting transfers between devices, shift(): high = lax.ppermute(low_part, axis, [(i + 1, i) for i in range(count - 1)])  3.88 us
    slice x1, local copies, waits for them, and re-layouts, cut_slab(): zlo, zhi = shift(field[..., :1], field[..., -1:], 'gz')  2.46 us
  transfers between devices with their start and end apart: 6, of which 3 were waited for; matrix products, arithmetic and copies ran while one was open for 15% of the time, Pallas kernels for 0%

profile of v1, /device:TPU:0, one launch (start us, length us, event | category | flops | bytes accessed | tf_op | source)
XLA Modules:
  0.0 116.5 jit_solution(7182646650491501597)
XLA Ops:
  0.6 2.5 %fusion.31 = (f32[3,32,32,1]{3,2,1,0:T(8,128)S(1)}, f32[3,32,32,1]{3,2,1,0:T(8,128)S(1)}) fusion(f32[3,32,32,256]{3,2,1,0:T(8,128)} %param.9), kind=kLoop, calls=%fused_computation.147 | loop fusion | bytes 49152 | tf_op jit(solution)/shard_map/slice | solution.py:204
  3.1 0.6 copy.127
  3.8 1.3 %collective-permute-start.1 = (f32[3,32,32,1]{2,1,3,0:T(8,128)S(1)}, f32[3,32,32,1]{2,1,3,0:T(8,128)S(1)}, u32[]{:S(2)}, u32[]{:S(2)}) collective-permute-start(f32[3,32,32,1]{2,1,3,0:T(8,128)S(1)} %copy.127), channel_id=1, source_target_pairs={{1,0},{3,2},{5,4},{7,6},{9,8},{11,10},{13,12},{15,14},{17,16},{19,... | collective-permute-start | bytes 36872 | tf_op jit(solution)/shard_map/ppermute | solution.py:198
  5.1 0.6 copy.126
  5.7 3.0 %collective-permute-start = (f32[3,32,32,1]{2,1,3,0:T(8,128)S(1)}, f32[3,32,32,1]{2,1,3,0:T(8,128)S(1)}, u32[]{:S(2)}, u32[]{:S(2)}) collective-permute-start(f32[3,32,32,1]{2,1,3,0:T(8,128)S(1)} %copy.126), channel_id=1, source_target_pairs={{0,1},{2,3},{4,5},{6,7},{8,9},{10,11},{12,13},{14,15},{16,17},{18,... | collective-permute-start | bytes 36872 | tf_op jit(solution)/shard_map/ppermute | solution.py:197
  8.7 1.0 fusion.30
  9.7 0.6 fusion.28
  10.4 0.7 fusion.27
  13.1 0.2 compare_reduce_fusion
  13.2 0.8 fusion.21
  14.0 0.2 select_reduce_fusion.1
  15.5 1.5 %constant_dynamic-slice_fusion.5 = f32[3,32,8,256]{3,2,1,0:T(8,128)S(1)} fusion(f32[3,32,32,256]{3,2,1,0:T(8,128)} %param.9, s32[]{:T(128)S(6)} %select_n.206), kind=kLoop, calls=%fused_computation.57 | loop fusion | bytes 1572868 | tf_op jit(solution)/shard_map/dynamic_slice | solution.py:215
  17.1 1.0 slice_bitcast_fusion.5
  19.3 2.2 %fusion.29 = (f32[3,32,1,256]{3,2,1,0:T(1,128)S(1)}, f32[3,32,1,256]{3,2,1,0:T(1,128)S(1)}, f32[3,32,1,256]{3,2,1,0:T(1,128)S(1)}, f32[3,32,1,256]{3,2,1,0:T(1,128)S(1)}) fusion(f32[3,32,32,256]{3,2,1,0:T(8,128)} %param.9, s32[]{:T(128)S(6)} %max.3, s32[]{:T(128)S(6)} %select_n.208), kind=kLoop, calls=%fused_computation.145 | loop fusion | bytes 786440 | tf_op jit(solution)/shard_map/dynamic_slice | solution.py:215
  21.5 0.8 select_select_fusion.tmat
  22.3 0.7 select_select_fusion.1.nmat
  22.9 1.9 %pad_add_fusion.at = s32[3]{0:T(128)} fusion(s32[1]{0:T(128)} %bitcast.28, s32[1]{0:T(128)} %bitcast.27, s32[1]{0:T(128)} %bitcast.26), kind=kLoop, calls=%fused_computation.126 | loop fusion | flops 6 | bytes 24 | tf_op jit(solution)/shard_map/stack | solution.py:322
  28.1 0.6 pad.9.planes
  28.7 1.1 concatenate.42.flags
  29.9 0.1 copy.92
  30.0 0.1 copy.91
  30.1 0.1 pad_maximum_fusion.3
  30.2 5.0 %collective-permute-start.2 = (f32[3,1,32,258]{3,2,1,0:T(8,128)S(1)}, f32[3,1,32,258]{3,2,1,0:T(8,128)S(1)}, u32[]{:S(2)}, u32[]{:S(2)}) collective-permute-start(f32[3,1,32,258]{3,2,1,0:T(8,128)S(1)} %pad_maximum_fusion.3), channel_id=1, source_target_pairs={{0,8},{8,16},{16,24},{1,9},{9,17},{17,25},{2,10},{10,18},{18,26},{... | collective-permute-start | bytes 297224 | tf_op jit(solution)/shard_map/ppermute | solution.py:197
  35.2 0.1 copy.97
  35.4 0.1 pad_maximum_fusion.4
  35.5 1.3 %collective-permute-start.3 = (f32[3,1,32,258]{3,2,1,0:T(8,128)S(1)}, f32[3,1,32,258]{3,2,1,0:T(8,128)S(1)}, u32[]{:S(2)}, u32[]{:S(2)}) collective-permute-start(f32[3,1,32,258]{3,2,1,0:T(8,128)S(1)} %pad_maximum_fusion.4), channel_id=1, source_target_pairs={{8,0},{16,8},{24,16},{9,1},{17,9},{25,17},{10,2},{18,10},{26,18},{... | collective-permute-start | bytes 297224 | tf_op jit(solution)/shard_map/ppermute | solution.py:198
  36.9 0.6 copy.105
  37.5 0.1 slice_bitcast_fusion.3
  37.6 0.1 slice_bitcast_fusion.2
  37.8 0.6 copy.106
  38.5 4.1 %collective-permute-done.3 = f32[3,1,32,258]{3,2,1,0:T(8,128)S(1)} collective-permute-done((f32[3,1,32,258]{3,2,1,0:T(8,128)S(1)}, f32[3,1,32,258]{3,2,1,0:T(8,128)S(1)}, u32[]{:S(2)}, u32[]{:S(2)}) %collective-permute-start.3) | collective-permute-done | bytes 99104 | tf_op jit(solution)/shard_map/ppermute | solution.py:198
  42.5 0.1 pad_maximum_fusion.2
  42.7 1.3 %collective-permute-start.5 = (f32[3,34,1,258]{3,1,2,0:T(8,128)S(1)}, f32[3,34,1,258]{3,1,2,0:T(8,128)S(1)}, u32[]{:S(2)}, u32[]{:S(2)}) collective-permute-start(f32[3,34,1,258]{3,1,2,0:T(8,128)S(1)} %pad_maximum_fusion.2), channel_id=1, source_target_pairs={{2,0},{4,2},{6,4},{3,1},{5,3},{7,5},{10,8},{12,10},{14,12},{11,9},... | collective-permute-start | bytes 315800 | tf_op jit(solution)/shard_map/ppermute | solution.py:198
  44.0 0.1 pad_maximum_fusion.1
  44.1 4.6 %collective-permute-start.4 = (f32[3,34,1,258]{3,1,2,0:T(8,128)S(1)}, f32[3,34,1,258]{3,1,2,0:T(8,128)S(1)}, u32[]{:S(2)}, u32[]{:S(2)}) collective-permute-start(f32[3,34,1,258]{3,1,2,0:T(8,128)S(1)} %pad_maximum_fusion.1), channel_id=1, source_target_pairs={{0,2},{2,4},{4,6},{1,3},{3,5},{5,7},{8,10},{10,12},{12,14},{9,11},... | collective-permute-start | bytes 315800 | tf_op jit(solution)/shard_map/ppermute | solution.py:197
  48.7 0.5 fusion.1
  49.2 1.7 %collective-permute-done.5 = f32[3,34,1,258]{3,1,2,0:T(8,128)S(1)} collective-permute-done((f32[3,34,1,258]{3,1,2,0:T(8,128)S(1)}, f32[3,34,1,258]{3,1,2,0:T(8,128)S(1)}, u32[]{:S(2)}, u32[]{:S(2)}) %collective-permute-start.5) | collective-permute-done | bytes 105296 | tf_op jit(solution)/shard_map/ppermute | solution.py:198
  50.9 0.2 fusion.6
  51.2 0.5 collective-permute-done.4
  51.7 0.2 fusion.11
  51.9 0.2 pad_maximum_fusion
  52.1 0.3 reshape.332
  52.4 0.6 pad.8.slab
  53.0 54.6 %fine_step.1 = (f32[3,4,16,256]{3,2,1,0:T(8,128)}, f32[4,16,128]{2,1,0:T(8,128)}) custom-call(s32[25]{0:T(128)} %concatenate.42.flags, f32[104,128]{1,0:T(8,128)} %pad.8.slab, f32[4,8,256]{2,1,0:T(8,128)} %pad.9.planes, f32[3,4,16,256]{3,2,1,0:T(8,128)} %fine.1, f32[4,16,256]{2,1,0:T(8,128)} %visc.1, f32[128,512]{1,0:T(8,128)} %constant.146.clone.kw, ...), custom_call_target="tpu_custom_call" | custom-call | tf_op jit(solution)/shard_map/fine_step/pallas_call | solution.py:296
  107.6 0.8 copy.123
  108.5 0.6 copy.124
  109.2 6.7 %coarse_fill.1 = f32[96,32,256]{2,1,0:T(8,128)} custom-call(s32[3]{0:T(128)} %pad_add_fusion.at, f32[96,32,256]{2,1,0:T(8,128)} %bitcast.97, f32[96,64]{1,0:T(8,128)} %bitcast.99), custom_call_target="tpu_custom_call" | custom-call | tf_op jit(solution)/shard_map/coarse_fill/pallas_call | solution.py:324
  115.8 0.7 copy.135
  (44 shorter events, 1.3 us)
Async XLA Ops:
  3.1 6.6 %copy-start.1 = (s32[64,3]{0,1:T(4,128)S(1)}, s32[64,3]{0,1:T(4,128)}, u32[]{:S(2)}) copy-start(s32[64,3]{0,1:T(4,128)} %param.12) | copy-start | bytes 2308
  3.1 7.2 %copy-start.2 = (s32[64]{0:T(128)S(1)}, s32[64]{0:T(128)}, u32[]{:S(2)}) copy-start(s32[64]{0:T(128)} %param.13) | copy-start | bytes 772
  3.1 9.9 %copy-start.3 = (s32[64,2]{0,1:T(2,128)S(1)}, s32[64,2]{0,1:T(2,128)}, u32[]{:S(2)}) copy-start(s32[64,2]{0,1:T(2,128)} %param.14) | copy-start | bytes 1540
  3.8 26.1 %collective-permute-start.1 = (f32[3,32,32,1]{2,1,3,0:T(8,128)S(1)}, f32[3,32,32,1]{2,1,3,0:T(8,128)S(1)}, u32[]{:S(2)}, u32[]{:S(2)}) collective-permute-start(f32[3,32,32,1]{2,1,3,0:T(8,128)S(1)} %copy.127), channel_id=1, source_target_pairs={{1,0},{3,2},{5,4},{7,6},{9,8},{11,10},{13,12},{15,14},{17,16},{19,... | collective-permute-start | bytes 36872 | tf_op jit(solution)/shard_map/ppermute | solution.py:198
  5.7 24.3 %collective-permute-start = (f32[3,32,32,1]{2,1,3,0:T(8,128)S(1)}, f32[3,32,32,1]{2,1,3,0:T(8,128)S(1)}, u32[]{:S(2)}, u32[]{:S(2)}) collective-permute-start(f32[3,32,32,1]{2,1,3,0:T(8,128)S(1)} %copy.126), channel_id=1, source_target_pairs={{0,1},{2,3},{4,5},{6,7},{8,9},{10,11},{12,13},{14,15},{16,17},{18,... | collective-permute-start | bytes 36872 | tf_op jit(solution)/shard_map/ppermute | solution.py:197
  30.2 8.2 %collective-permute-start.2 = (f32[3,1,32,258]{3,2,1,0:T(8,128)S(1)}, f32[3,1,32,258]{3,2,1,0:T(8,128)S(1)}, u32[]{:S(2)}, u32[]{:S(2)}) collective-permute-start(f32[3,1,32,258]{3,2,1,0:T(8,128)S(1)} %pad_maximum_fusion.3), channel_id=1, source_target_pairs={{0,8},{8,16},{16,24},{1,9},{9,17},{17,25},{2,10},{10,18},{18,26},{... | collective-permute-start | bytes 297224 | tf_op jit(solution)/shard_map/ppermute | solution.py:197
  35.5 7.0 %collective-permute-start.3 = (f32[3,1,32,258]{3,2,1,0:T(8,128)S(1)}, f32[3,1,32,258]{3,2,1,0:T(8,128)S(1)}, u32[]{:S(2)}, u32[]{:S(2)}) collective-permute-start(f32[3,1,32,258]{3,2,1,0:T(8,128)S(1)} %pad_maximum_fusion.4), channel_id=1, source_target_pairs={{8,0},{16,8},{24,16},{9,1},{17,9},{25,17},{10,2},{18,10},{26,18},{... | collective-permute-start | bytes 297224 | tf_op jit(solution)/shard_map/ppermute | solution.py:198
  42.7 8.3 %collective-permute-start.5 = (f32[3,34,1,258]{3,1,2,0:T(8,128)S(1)}, f32[3,34,1,258]{3,1,2,0:T(8,128)S(1)}, u32[]{:S(2)}, u32[]{:S(2)}) collective-permute-start(f32[3,34,1,258]{3,1,2,0:T(8,128)S(1)} %pad_maximum_fusion.2), channel_id=1, source_target_pairs={{2,0},{4,2},{6,4},{3,1},{5,3},{7,5},{10,8},{12,10},{14,12},{11,9},... | collective-permute-start | bytes 315800 | tf_op jit(solution)/shard_map/ppermute | solution.py:198
  44.1 7.6 %collective-permute-start.4 = (f32[3,34,1,258]{3,1,2,0:T(8,128)S(1)}, f32[3,34,1,258]{3,1,2,0:T(8,128)S(1)}, u32[]{:S(2)}, u32[]{:S(2)}) collective-permute-start(f32[3,34,1,258]{3,1,2,0:T(8,128)S(1)} %pad_maximum_fusion.1), channel_id=1, source_target_pairs={{0,2},{2,4},{4,6},{1,3},{3,5},{5,7},{8,10},{10,12},{12,14},{9,11},... | collective-permute-start | bytes 315800 | tf_op jit(solution)/shard_map/ppermute | solution.py:197
  109.2 6.7 %copy-start = (f32[3,4,16,256]{3,2,1,0:T(8,128)S(1)}, f32[3,4,16,256]{3,2,1,0:T(8,128)}, u32[]{:S(2)}) copy-start(f32[3,4,16,256]{3,2,1,0:T(8,128)} %get-tuple-element.67) | copy-start | bytes 589828

commit v2 on v1

--- a/solution.py
+++ b/solution.py
@@ -12,7 +12,9 @@
 SLOTS = 4
 SIDE = B + 2
 LANES = 128
-MEAN_ROWS = 16
+MEAN_ROWS = 12
+PLANES = 4
+PLANE_ROWS = 6
 step_rate = 0.15
 HIGHEST = lax.Precision.HIGHEST
 
@@ -32,17 +34,35 @@
     return tangent, low, low[::-1].copy()
 
 
-def ghost_matrix():
+def edge_matrices(nx):
     tangent, low, high = tables()
-    out = np.zeros((LANES, 2 * F * F), np.float32)
-    edge = np.zeros((SIDE, SIDE, F, F), np.float32)
-    edge[:, :, 0, :] += np.einsum("b,tc->bct", low, tangent)
-    edge[:, :, F - 1, :] += np.einsum("b,tc->bct", high, tangent)
-    edge[:, :, :, 0] += np.einsum("sb,c->bcs", tangent, low)
-    edge[:, :, :, F - 1] += np.einsum("sb,c->bcs", tangent, high)
-    out[: SIDE * SIDE, : F * F] = edge.reshape(SIDE * SIDE, F * F)
-    out[: SIDE * SIDE, F * F :] = np.einsum("sb,tc->bcst", tangent, tangent).reshape(SIDE * SIDE, F * F)
-    return out
+    eye = np.eye(SIDE, dtype=np.float32)
+    wide = 4 * SIDE
+    cut = np.zeros((SIDE, SIDE, 4, SIDE), np.float32)
+    cut[:, :, 0] = np.einsum("b,cd->bcd", low, eye)
+    cut[:, :, 1] = np.einsum("b,cd->bcd", high, eye)
+    cut[:, :, 2] = np.einsum("bd,c->bcd", eye, low)
+    cut[:, :, 3] = np.einsum("bd,c->bcd", eye, high)
+    put = np.zeros((4, SIDE, F, F), np.float32)
+    put[0, :, 0, :] = tangent.T
+    put[1, :, F - 1, :] = tangent.T
+    put[2, :, :, 0] = tangent.T
+    put[3, :, :, F - 1] = tangent.T
+    rows = up(3 * nx, 8)
+    edge_rows = up(nx + 6, 8)
+    columns = np.zeros((3, LANES, LANES), np.float32)
+    places = np.zeros((3, LANES, F * F), np.float32)
+    lines = np.zeros((4, edge_rows, rows), np.float32)
+    for k in range(3):
+        columns[k, : SIDE * SIDE, k * wide : (k + 1) * wide] = cut.reshape(SIDE * SIDE, wide)
+        places[k, k * wide : (k + 1) * wide] = put.reshape(wide, F * F)
+        lines[k, np.arange(nx), k * nx + np.arange(nx)] = 1.0
+        for row, outer, inner in ((0, 0, 1), (1, nx - 1, nx - 2)):
+            lines[3, nx + 2 * k + row, k * nx + outer] = 0.75
+            lines[3, nx + 2 * k + row, k * nx + inner] = 0.25
+    across = np.zeros((LANES, F * F), np.float32)
+    across[: SIDE * SIDE] = np.einsum("sb,tc->bcst", tangent, tangent).reshape(SIDE * SIDE, F * F)
+    return columns, lines, places, across
 
 
 def mean_matrices():
@@ -66,8 +86,24 @@
     return jnp.dot(a, b, precision=HIGHEST, preferred_element_type=jnp.float32)
 
 
+def edge_kernel(chosen, slab, fine, columns, lines, edges, planes):
+    total = dot(lines[3], slab[...])
+    for k in range(3):
+        total += dot(lines[k], dot(slab[...], columns[k]))
+    edges[...] = total
+    for p in range(PLANES):
+        slot = chosen[p] // 2
+        low_side = chosen[p] % 2 == 0
+        for k in range(3):
+            v = fine[k, slot]
+            line = jnp.where(low_side, v[F - 1 : F], v[0:1])
+            for h in range(2):
+                at = p * PLANE_ROWS + k * 2 + h
+                planes[at : at + 1] = line[:, h * LANES : (h + 1) * LANES]
+
+
 def fine_kernel(
-    nx, ny, flags, slab, planes, fine, visc, kw, tmat, nmat, lane_mean, row_mean,
+    nx, ny, width, flags, edges, planes, fine, visc, places, across, lane_mean, row_mean,
     fine_out, picked, slabs, plane_buf, mean_send, means, advs, send_sem, recv_sem, own_sem,
 ):
     count = nx * ny
@@ -84,13 +120,13 @@
         )
 
     def slab_copy(o):
-        return remote(o, 0, slab, slabs.at[me])
+        return remote(o, 0, edges, slabs.at[me])
 
     def plane_copy(o):
-        return remote(o, 1, planes, plane_buf.at[pl.ds(me * SLOTS, SLOTS)])
+        return remote(o, 1, planes, plane_buf.at[me])
 
     def mean_copy(o):
-        return remote(o, 2, mean_send, means.at[pl.ds(me * SLOTS, SLOTS)])
+        return remote(o, 2, mean_send, means.at[me])
 
     barrier = pltpu.get_barrier_semaphore()
 
@@ -99,8 +135,8 @@
         return c
 
     lax.fori_loop(1, count, greet, 0)
-    own_slab = pltpu.make_async_copy(slab, slabs.at[me], own_sem.at[0])
-    own_plane = pltpu.make_async_copy(planes, plane_buf.at[pl.ds(me * SLOTS, SLOTS)], own_sem.at[1])
+    own_slab = pltpu.make_async_copy(edges, slabs.at[me], own_sem.at[0])
+    own_plane = pltpu.make_async_copy(planes, plane_buf.at[me], own_sem.at[1])
     own_slab.start()
     own_plane.start()
     pl.semaphore_wait(barrier, count - 1)
@@ -121,23 +157,48 @@
 
     lax.fori_loop(1, count, finish, 0)
 
-    half = dot(slabs[flags[0]], kw[...])
-    ghost = dot(tmat[...], half[:, : F * F])
-    xface = dot(nmat[...], half[:, F * F :])
+    def flag(group, s):
+        return flags[1 + group * SLOTS + s]
+
+    mine = slabs[flags[0]]
+    shape = (SLOTS * F, mine.shape[0])
+    line_id = lax.broadcasted_iota(jnp.int32, shape, 0)
+    from_row = lax.broadcasted_iota(jnp.int32, shape, 1)
+    box = jnp.full(shape, flag(1, 0), jnp.int32)
+    for s in range(1, SLOTS):
+        box = jnp.where(line_id // F == s, flag(1, s), box)
+    i_id = line_id % F
+    center = B * box + i_id // 2 + 1
+    other = jnp.where(i_id % 2 == 0, center - 1, center + 1)
+    blend = jnp.where(from_row == center, 0.75, jnp.where(from_row == other, 0.25, 0.0))
+    along = dot(blend, mine)
+    ghosts = [dot(along, places[k]) for k in range(3)]
+    xface = dot(mine, across[...])[width : width + 6]
     lane = lax.broadcasted_iota(jnp.int32, (F, F * F), 1)
     row = lax.broadcasted_iota(jnp.int32, (F, F * F), 0)
     lz = lane % F
     for s in range(SLOTS):
-        active = flags[1 + s] > 0
-        low_near = plane_buf[flags[1 + SLOTS + s]]
-        high_near = plane_buf[flags[1 + 2 * SLOTS + s]]
-        has_low = flags[1 + 3 * SLOTS + s] > 0
-        has_high = flags[1 + 4 * SLOTS + s] > 0
+        active = flag(0, s) > 0
+        near = []
+        for side in range(2):
+            base = 2 + 5 * side
+            far = plane_buf[flag(base, s)]
+            rank = flag(base + 1, s)
+            chosen = far[:PLANE_ROWS]
+            for p in range(1, PLANES):
+                chosen = jnp.where(rank == p, far[p * PLANE_ROWS : (p + 1) * PLANE_ROWS], chosen)
+            near.append((chosen, flag(base + 2, s), flag(base + 3, s) > 0, flag(base + 4, s) > 0))
         for k in range(3):
             v = fine[k, s]
-            r = (k * SLOTS + s) * 2
-            lower = jnp.where(has_low, low_near[2 * k : 2 * k + 1], xface[r : r + 1])
-            upper = jnp.where(has_high, high_near[2 * k + 1 : 2 * k + 2], xface[r + 1 : r + 2])
+            ends = []
+            for side in range(2):
+                chosen, slot, local, has = near[side]
+                x = (F - 1) * (1 - side)
+                far = jnp.concatenate([chosen[2 * k : 2 * k + 1], chosen[2 * k + 1 : 2 * k + 2]], axis=1)
+                here = fine[k, slot][x : x + 1]
+                outer = xface[2 * k + side : 2 * k + side + 1]
+                ends.append(jnp.where(has, jnp.where(local, here, far), outer))
+            lower, upper = ends
             total = jnp.where(row == 0, lower, pltpu.roll(v, 1, 0))
             total += jnp.where(row == F - 1, upper, pltpu.roll(v, F - 1, 0))
             total += jnp.where(lane < F, 0.0, pltpu.roll(v, F, 1))
@@ -145,7 +206,7 @@
             total += jnp.where(lz == 0, 0.0, pltpu.roll(v, 1, 1))
             total += jnp.where(lz == F - 1, 0.0, pltpu.roll(v, F * F - 1, 1))
             at = (k * SLOTS + s) * F
-            total += ghost[at : at + F] - 6.0 * v
+            total += ghosts[k][s * F : s * F + F] - 6.0 * v
             adv = v + step_rate * visc[s] * total
             advs[at : at + F] = adv
             fine_out[k, s] = jnp.where(active, adv, 0.0)
@@ -153,10 +214,9 @@
     first = dot(row_mean[0], z)
     second = dot(row_mean[1], z)
     lane_m = lax.broadcasted_iota(jnp.int32, first.shape, 1)
-    packed = jnp.where(lane_m < 64, first, second).reshape(SLOTS, MEAN_ROWS, LANES)
+    packed = jnp.where(lane_m < 64, first, second)
     mean_send[...] = packed
-    for s in range(SLOTS):
-        means[me * SLOTS + s] = packed[s]
+    means[me] = packed
 
     def send_mean(o, c):
         mean_copy(o).start()
@@ -170,7 +230,12 @@
 
     lax.fori_loop(1, count, finish_mean, 0)
     for s in range(SLOTS):
-        picked[s] = means[flags[1 + 5 * SLOTS + s]]
+        got = means[flag(12, s)]
+        part = flag(13, s)
+        value = got[:MEAN_ROWS]
+        for p in range(1, SLOTS):
+            value = jnp.where(part == p, got[p * MEAN_ROWS : (p + 1) * MEAN_ROWS], value)
+        picked[s] = value
 
 
 def coarse_kernel(at, field, rows, out):
@@ -245,7 +310,10 @@
     home_z = corners[:, 2] // brick_z
     in_brick = (home_x == index_x) & (home_y == index_y) & (home_z == index_z)
     box_x = (corners[:, 0] - home_x * brick_x) // B
-    owner_row = grid_slot // (SLOTS * count_z) * SLOTS + grid_slot % SLOTS
+    owner_group = grid_slot // (SLOTS * count_z)
+    owner_slot = grid_slot % SLOTS
+    owner_dev = grid_slot // SLOTS
+    grid_ids = jnp.arange(corners.shape[0], dtype=jnp.int32)
 
     def pick(match, values):
         return jnp.sum(jnp.where(match, values[None, :], 0), axis=1)
@@ -254,58 +322,73 @@
     anchor_y = jnp.max(jnp.where(in_brick, corners[:, 1] - index_y * brick_y, 0))
     anchor_z = jnp.max(jnp.where(in_brick, corners[:, 2] - index_z * brick_z, 0))
     row_match = in_brick[None, :] & (box_x[None, :] == slot_range[:, None])
-    need_mean = pick(row_match, owner_row)
+    need_mean = pick(row_match, grid_slot)
     own_match = grid_slot[None, :] == (my_device * SLOTS + slot_range)[:, None]
     active = jnp.any(own_match, axis=1)
     slot_box = pick(own_match, box_x)
     home = jnp.max(jnp.where(own_match, (home_x * count_y + home_y)[None, :], 0))
     near_low = pick(own_match, neighbors[:, 0])
     near_high = pick(own_match, neighbors[:, 1])
-    has_low = active & (near_low >= 0)
-    has_high = active & (near_high >= 0)
-    grid_ids = jnp.arange(corners.shape[0], dtype=jnp.int32)
-    low_row = pick(grid_ids[None, :] == near_low[:, None], owner_row)
-    high_row = pick(grid_ids[None, :] == near_high[:, None], owner_row)
-    flags = jnp.concatenate(
-        [home[None], active.astype(jnp.int32), low_row, high_row,
-         has_low.astype(jnp.int32), has_high.astype(jnp.int32), need_mean]
-    ).astype(jnp.int32)
+
+    leaves = []
+    for side in range(2):
+        near_all = neighbors[:, 1 - side]
+        near_dev = pick(grid_ids[None, :] == near_all[:, None], owner_dev)
+        leaves.append((near_all >= 0) & (near_dev != owner_dev))
+    same = owner_dev[None, :] == owner_dev[:, None]
+    ahead = same & (owner_slot[None, :] < owner_slot[:, None])
+    before = pick(ahead, leaves[0].astype(jnp.int32) + leaves[1].astype(jnp.int32))
+    ranks = (before, before + leaves[0].astype(jnp.int32))
+    own = owner_dev == my_device
+    plane_range = jnp.arange(PLANES, dtype=jnp.int32)
+    chosen = jnp.zeros((PLANES,), jnp.int32)
+    for side in range(2):
+        match = (own & leaves[side])[None, :] & (ranks[side][None, :] == plane_range[:, None])
+        chosen = chosen + pick(match, owner_slot * 2 + side)
+    parts = [home[None], active.astype(jnp.int32), slot_box]
+    for side, near in ((0, near_low), (1, near_high)):
+        match = grid_ids[None, :] == near[:, None]
+        local = pick(match, owner_dev) == my_device
+        parts += [
+            pick(match, owner_group),
+            pick(match, ranks[side]),
+            pick(match, owner_slot),
+            local.astype(jnp.int32),
+            (active & (near >= 0)).astype(jnp.int32),
+        ]
+    parts += [need_mean // (SLOTS * count_z), need_mean % SLOTS]
+    flags = jnp.concatenate(parts).astype(jnp.int32)
 
     slab = cut_slab(coarse_field, anchor_y, anchor_z)
-    slab_rows = slab.shape[0]
-    planes = jnp.stack([fine_field[:, :, F - 1, :], fine_field[:, :, 0, :]], axis=1)
-    planes = planes.reshape(6, SLOTS, F * F).transpose(1, 0, 2)
-    planes = jnp.pad(planes, ((0, 0), (0, 2), (0, 0)))
-
-    k_id = jnp.arange(3, dtype=jnp.int32)[:, None, None, None]
-    i_id = jnp.arange(F, dtype=jnp.int32)[None, None, :, None]
-    r_id = jnp.arange(slab_rows, dtype=jnp.int32)[None, None, None, :]
-    base = k_id * (brick_x + 2) + B * slot_box[None, :, None, None]
-    center = i_id // 2 + 1
-    other = jnp.where(i_id % 2 == 0, center - 1, center + 1)
-    tmat = jnp.where(r_id == base + center, 0.75, jnp.where(r_id == base + other, 0.25, 0.0))
-    tmat = tmat.reshape(3 * SLOTS * F, slab_rows).astype(jnp.float32)
-    side_id = jnp.arange(2, dtype=jnp.int32)[None, None, :, None]
-    outer = jnp.where(side_id == 0, 0, SIDE - 1)
-    inner = jnp.where(side_id == 0, 1, SIDE - 2)
-    nmat = jnp.where(r_id == base + outer, 0.75, jnp.where(r_id == base + inner, 0.25, 0.0))
-    nmat = nmat.reshape(3 * SLOTS * 2, slab_rows).astype(jnp.float32)
+    columns, lines, places, across = edge_matrices(brick_x + 2)
+    edge_rows = lines.shape[1]
+    vmem = pl.BlockSpec(memory_space=pltpu.VMEM)
+    smem = pl.BlockSpec(memory_space=pltpu.SMEM)
+    edges, planes = pl.pallas_call(
+        edge_kernel,
+        out_shape=(
+            jax.ShapeDtypeStruct((edge_rows, LANES), jnp.float32),
+            jax.ShapeDtypeStruct((PLANES * PLANE_ROWS, LANES), jnp.float32),
+        ),
+        in_specs=[smem] + [vmem] * 4,
+        out_specs=(vmem, vmem),
+        name="edge_cut",
+    )(chosen, slab, fine_field, jnp.asarray(columns), jnp.asarray(lines))
 
     lane_mean, row_mean = mean_matrices()
-    vmem = pl.BlockSpec(memory_space=pltpu.VMEM)
     fine_out, picked = pl.pallas_call(
-        functools.partial(fine_kernel, count_x, count_y),
+        functools.partial(fine_kernel, count_x, count_y, brick_x + 2),
         out_shape=(
             jax.ShapeDtypeStruct(fine_field.shape, jnp.float32),
             jax.ShapeDtypeStruct((SLOTS, MEAN_ROWS, LANES), jnp.float32),
         ),
-        in_specs=[pl.BlockSpec(memory_space=pltpu.SMEM)] + [vmem] * 9,
+        in_specs=[smem] + [vmem] * 8,
         out_specs=(vmem, vmem),
         scratch_shapes=[
-            pltpu.VMEM((count, slab_rows, LANES), jnp.float32),
-            pltpu.VMEM((count * SLOTS, 8, F * F), jnp.float32),
-            pltpu.VMEM((SLOTS, MEAN_ROWS, LANES), jnp.float32),
-            pltpu.VMEM((count * SLOTS, MEAN_ROWS, LANES), jnp.float32),
+            pltpu.VMEM((count, edge_rows, LANES), jnp.float32),
+            pltpu.VMEM((count, PLANES * PLANE_ROWS, LANES), jnp.float32),
+            pltpu.VMEM((SLOTS * MEAN_ROWS, LANES), jnp.float32),
+            pltpu.VMEM((count, SLOTS * MEAN_ROWS, LANES), jnp.float32),
             pltpu.VMEM((3 * SLOTS * F, F * F), jnp.float32),
             pltpu.SemaphoreType.DMA((3, count)),
             pltpu.SemaphoreType.DMA((3, count)),
@@ -314,7 +397,7 @@
         compiler_params=pltpu.CompilerParams(collective_id=0, has_side_effects=True),
         name="fine_step",
     )(
-        flags, slab, planes, fine_field, viscosity, jnp.asarray(ghost_matrix()), tmat, nmat,
+        flags, edges, planes, fine_field, viscosity, jnp.asarray(places), jnp.asarray(across),
         jnp.asarray(lane_mean), jnp.asarray(row_mean),
     )
     rows = picked[:, : 3 * (B // 2)].reshape(SLOTS, 3, B // 2, 2, B * B)

time: 117 us -> 92.3 us (0.79)
  Pallas kernels: 61.3 us -> 38.9 us
  local copies, waits for them, and re-layouts: 16.8 us -> 15.1 us
    pallas_call x1 -> x2, Pallas kernels: 54.6 us -> 32.2 us  [the longest x1 29.5 us: on_device(): pl.pallas_call(functools.partial(fine_kernel, count_x, count_y, brick_x +...]
    select_n x4 -> x1, other arithmetic: 1.44 us -> 0.01 us  [on_device(): parts += [need_mean // (SLOTS * count_z), need_mean % SLOTS]]
  transfers between devices with their start and end apart: 6 -> 6, of which waited for: 3 -> 3; matrix products, arithmetic and copies ran while one was open for 15% -> 16% of each run, Pallas kernels for 0% -> 0%
where the time goes in v2:
time: 92.3 us; the launch traced here: 91.5 us
  Pallas kernels  38.9 us (42%)
  starting transfers between devices  16.4 us (18%)
  local copies, waits for them, and re-layouts  15.1 us (16%)
  between operations  7.89 us (9%)
  other arithmetic  6.91 us (7%)
  waiting for transfers between devices  6.32 us (7%)
    pallas_call x1, Pallas kernels, on_device(): pl.pallas_call(functools.partial(fine_kernel, count_x, count_y, brick_x +...  29.5 us
    ppermute x3, starting transfers between devices, shift(): low = lax.ppermute(high_part, axis, [(i, i + 1) for i in range(count - 1)])  12.6 us
    pallas_call x1, Pallas kernels, on_device(): pl.pallas_call(coarse_kernel, out_shape=jax.ShapeDtypeStruct((3 * brick_x...  6.68 us
    ppermute x3, waiting for transfers between devices, shift(): high = lax.ppermute(low_part, axis, [(i + 1, i) for i in range(count - 1)])  5.77 us
    dynamic_slice x12, local copies, waits for them, and re-layouts, cut(): return lax.dynamic_slice_in_dim(a, start, size, axis=2)  5.4 us
    ppermute x3, starting transfers between devices, shift(): high = lax.ppermute(low_part, axis, [(i + 1, i) for i in range(count - 1)])  3.88 us
    pallas_call x1, Pallas kernels, on_device(): pl.pallas_call(edge_kernel, out_shape=(jax.ShapeDtypeStruct((edge_rows, L...  2.65 us
    slice x1, local copies, waits for them, and re-layouts, cut_slab(): zlo, zhi = shift(field[..., :1], field[..., -1:], 'gz')  2.46 us
  transfers between devices with their start and end apart: 6, of which 3 were waited for; matrix products, arithmetic and copies ran while one was open for 16% of the time, Pallas kernels for 0%

profile of v2, /device:TPU:0, one launch (start us, length us, event | category | flops | bytes accessed | tf_op | source)
XLA Modules:
  0.0 91.5 jit_solution(13194870859318350564)
XLA Ops:
  0.6 2.5 %fusion.32 = (f32[3,32,32,1]{3,2,1,0:T(8,128)S(1)}, f32[3,32,32,1]{3,2,1,0:T(8,128)S(1)}) fusion(f32[3,32,32,256]{3,2,1,0:T(8,128)} %param.12), kind=kLoop, calls=%fused_computation.156 | loop fusion | bytes 49152 | tf_op jit(solution)/shard_map/slice | solution.py:269
  3.1 0.6 copy.121
  3.8 1.3 %collective-permute-start.1 = (f32[3,32,32,1]{2,1,3,0:T(8,128)S(1)}, f32[3,32,32,1]{2,1,3,0:T(8,128)S(1)}, u32[]{:S(2)}, u32[]{:S(2)}) collective-permute-start(f32[3,32,32,1]{2,1,3,0:T(8,128)S(1)} %copy.121), channel_id=1, source_target_pairs={{1,0},{3,2},{5,4},{7,6},{9,8},{11,10},{13,12},{15,14},{17,16},{19,... | collective-permute-start | bytes 36872 | tf_op jit(solution)/shard_map/ppermute | solution.py:263
  5.1 0.6 copy.120
  5.7 3.0 %collective-permute-start = (f32[3,32,32,1]{2,1,3,0:T(8,128)S(1)}, f32[3,32,32,1]{2,1,3,0:T(8,128)S(1)}, u32[]{:S(2)}, u32[]{:S(2)}) collective-permute-start(f32[3,32,32,1]{2,1,3,0:T(8,128)S(1)} %copy.120), channel_id=1, source_target_pairs={{0,1},{2,3},{4,5},{6,7},{8,9},{10,11},{12,13},{14,15},{16,17},{18,... | collective-permute-start | bytes 36872 | tf_op jit(solution)/shard_map/ppermute | solution.py:262
  8.7 1.0 %fusion.31 = (f32[3,1,32,256]{3,2,1,0:T(8,128)S(1)}, f32[3,1,32,256]{3,2,1,0:T(8,128)S(1)}) fusion(f32[3,32,32,256]{3,2,1,0:T(8,128)} %param.12), kind=kLoop, calls=%fused_computation.155 | loop fusion | bytes 393216 | tf_op jit(solution)/shard_map/slice | solution.py:274
  9.8 0.2 select_reduce_fusion.1
  10.0 0.6 compare_and_fusion.4
  10.6 0.6 fusion.28
  13.2 0.2 compare_reduce_fusion
  13.4 0.2 select_reduce_fusion
  13.6 0.9 select_reduce_fusion.5
  14.5 0.3 select_reduce_fusion.3
  16.1 1.5 %constant_dynamic-slice_fusion.5 = f32[3,32,8,256]{3,2,1,0:T(8,128)S(1)} fusion(f32[3,32,32,256]{3,2,1,0:T(8,128)} %param.12, s32[]{:T(128)S(6)} %select_n.198), kind=kLoop, calls=%fused_computation.52 | loop fusion | bytes 1572868 | tf_op jit(solution)/shard_map/dynamic_slice | solution.py:280
  18.3 2.2 %fusion.30 = (f32[3,32,1,256]{3,2,1,0:T(1,128)S(1)}, f32[3,32,1,256]{3,2,1,0:T(1,128)S(1)}, f32[3,32,1,256]{3,2,1,0:T(1,128)S(1)}, f32[3,32,1,256]{3,2,1,0:T(1,128)S(1)}) fusion(f32[3,32,32,256]{3,2,1,0:T(8,128)} %param.12, s32[]{:T(128)S(6)} %max.3, s32[]{:T(128)S(6)} %select_n.200), kind=kLoop, calls=%fused_computation.154 | loop fusion | bytes 786440 | tf_op jit(solution)/shard_map/dynamic_slice | solution.py:280
  20.5 1.8 %pad_add_fusion.at = s32[3]{0:T(128)} fusion(s32[1]{0:T(128)} %bitcast.24, s32[1]{0:T(128)} %bitcast.23, s32[1]{0:T(128)} %bitcast.22), kind=kLoop, calls=%fused_computation.133 | loop fusion | flops 6 | bytes 24 | tf_op jit(solution)/shard_map/stack | solution.py:405
  24.8 0.5 add.122.chosen
  25.9 1.4 %concatenate.42.flags = s32[57]{0:T(128)} concatenate(s32[1]{0:T(128)} %bitcast.2, s32[4]{0:T(128)S(1)} %get-tuple-element.74, s32[4]{0:T(128)S(1)} %get-tuple-element.13, s32[4]{0:T(128)S(1)} %get-tuple-element.25, s32[4]{0:T(128)S(1)} %get-tuple-element.23, s32[4]{0:T(128)S(1)} %get-tuple-element.21, s32[4]{0:T(128)S(1)} %compare_convert_fusion.1, s32[4]{0:T(128)S(1)} %get-tuple-element.73, ...), dimensions={0} | concatenate | bytes 456 | tf_op jit(solution)/shard_map/concatenate | solution.py:360
  27.3 0.1 copy.88
  27.4 0.1 copy.87
  27.5 0.1 pad_maximum_fusion.3
  27.6 5.0 %collective-permute-start.2 = (f32[3,1,32,258]{3,2,1,0:T(8,128)S(1)}, f32[3,1,32,258]{3,2,1,0:T(8,128)S(1)}, u32[]{:S(2)}, u32[]{:S(2)}) collective-permute-start(f32[3,1,32,258]{3,2,1,0:T(8,128)S(1)} %pad_maximum_fusion.3), channel_id=1, source_target_pairs={{0,8},{8,16},{16,24},{1,9},{9,17},{17,25},{2,10},{10,18},{18,26},{... | collective-permute-start | bytes 297224 | tf_op jit(solution)/shard_map/ppermute | solution.py:262
  32.6 0.1 copy.93
  32.8 0.1 pad_maximum_fusion.4
  32.9 1.3 %collective-permute-start.3 = (f32[3,1,32,258]{3,2,1,0:T(8,128)S(1)}, f32[3,1,32,258]{3,2,1,0:T(8,128)S(1)}, u32[]{:S(2)}, u32[]{:S(2)}) collective-permute-start(f32[3,1,32,258]{3,2,1,0:T(8,128)S(1)} %pad_maximum_fusion.4), channel_id=1, source_target_pairs={{8,0},{16,8},{24,16},{9,1},{17,9},{25,17},{10,2},{18,10},{26,18},{... | collective-permute-start | bytes 297224 | tf_op jit(solution)/shard_map/ppermute | solution.py:263
  34.3 0.6 copy.101
  34.9 0.1 slice_bitcast_fusion.3
  35.0 0.1 slice_bitcast_fusion.2
  35.2 0.6 copy.102
  35.9 4.1 %collective-permute-done.3 = f32[3,1,32,258]{3,2,1,0:T(8,128)S(1)} collective-permute-done((f32[3,1,32,258]{3,2,1,0:T(8,128)S(1)}, f32[3,1,32,258]{3,2,1,0:T(8,128)S(1)}, u32[]{:S(2)}, u32[]{:S(2)}) %collective-permute-start.3) | collective-permute-done | bytes 99104 | tf_op jit(solution)/shard_map/ppermute | solution.py:263
  39.9 0.1 pad_maximum_fusion.2
  40.1 1.3 %collective-permute-start.5 = (f32[3,34,1,258]{3,1,2,0:T(8,128)S(1)}, f32[3,34,1,258]{3,1,2,0:T(8,128)S(1)}, u32[]{:S(2)}, u32[]{:S(2)}) collective-permute-start(f32[3,34,1,258]{3,1,2,0:T(8,128)S(1)} %pad_maximum_fusion.2), channel_id=1, source_target_pairs={{2,0},{4,2},{6,4},{3,1},{5,3},{7,5},{10,8},{12,10},{14,12},{11,9},... | collective-permute-start | bytes 315800 | tf_op jit(solution)/shard_map/ppermute | solution.py:263
  41.4 0.1 pad_maximum_fusion.1
  41.5 4.6 %collective-permute-start.4 = (f32[3,34,1,258]{3,1,2,0:T(8,128)S(1)}, f32[3,34,1,258]{3,1,2,0:T(8,128)S(1)}, u32[]{:S(2)}, u32[]{:S(2)}) collective-permute-start(f32[3,34,1,258]{3,1,2,0:T(8,128)S(1)} %pad_maximum_fusion.1), channel_id=1, source_target_pairs={{0,2},{2,4},{4,6},{1,3},{3,5},{5,7},{8,10},{10,12},{12,14},{9,11},... | collective-permute-start | bytes 315800 | tf_op jit(solution)/shard_map/ppermute | solution.py:262
  46.1 0.5 fusion.1
  46.6 1.7 %collective-permute-done.5 = f32[3,34,1,258]{3,1,2,0:T(8,128)S(1)} collective-permute-done((f32[3,34,1,258]{3,1,2,0:T(8,128)S(1)}, f32[3,34,1,258]{3,1,2,0:T(8,128)S(1)}, u32[]{:S(2)}, u32[]{:S(2)}) %collective-permute-start.5) | collective-permute-done | bytes 105296 | tf_op jit(solution)/shard_map/ppermute | solution.py:263
  48.3 0.2 fusion.6
  48.6 0.5 collective-permute-done.4
  49.1 0.2 fusion.11
  49.3 0.2 pad_maximum_fusion
  49.5 0.3 reshape.184
  49.8 0.6 pad.4.slab
  50.4 2.7 %edge_cut.1 = (f32[40,128]{1,0:T(8,128)}, f32[24,128]{1,0:T(8,128)}) custom-call(s32[4]{0:T(128)} %add.122.chosen, f32[104,128]{1,0:T(8,128)} %pad.4.slab, f32[3,4,16,256]{3,2,1,0:T(8,128)} %fine.3, f32[3,128,128]{2,1,0:T(8,128)} %constant.138.clone.columns, f32[4,40,104]{2,1,0:T(8,128)} %constant.139.clone.lines), custom_call_target="tpu_custom_call" | custom-call | tf_op jit(solution)/shard_map/edge_cut/pallas_call | solution.py:367
  53.1 29.5 %fine_step.1 = (f32[3,4,16,256]{3,2,1,0:T(8,128)}, f32[4,12,128]{2,1,0:T(8,128)}) custom-call(s32[57]{0:T(128)} %concatenate.42.flags, f32[40,128]{1,0:T(8,128)} %get-tuple-element.6.edges, f32[24,128]{1,0:T(8,128)} %get-tuple-element.7.planes, f32[3,4,16,256]{3,2,1,0:T(8,128)} %fine.3, f32[4,16,256]{2,1,0:T(8,128)} %visc.1, ...), custom_call_target="tpu_custom_call" | custom-call | tf_op jit(solution)/shard_map/fine_step/pallas_call | solution.py:379
  82.6 0.8 copy.117
  83.5 0.6 copy.118
  84.2 6.7 %coarse_fill.1 = f32[96,32,256]{2,1,0:T(8,128)} custom-call(s32[3]{0:T(128)} %pad_add_fusion.at, f32[96,32,256]{2,1,0:T(8,128)} %bitcast.97, f32[96,64]{1,0:T(8,128)} %bitcast.99), custom_call_target="tpu_custom_call" | custom-call | tf_op jit(solution)/shard_map/coarse_fill/pallas_call | solution.py:407
  90.8 0.7 copy.127
  (37 shorter events, 0.7 us)
Async XLA Ops:
  3.1 6.6 %copy-start.3 = (s32[64]{0:T(128)S(1)}, s32[64]{0:T(128)}, u32[]{:S(2)}) copy-start(s32[64]{0:T(128)} %param.16) | copy-start | bytes 772
  3.1 6.6 %copy-start.1 = (s32[64,2]{0,1:T(2,128)S(1)}, s32[64,2]{0,1:T(2,128)}, u32[]{:S(2)}) copy-start(s32[64,2]{0,1:T(2,128)} %param.17) | copy-start | bytes 1540
  3.1 6.8 %copy-start.2 = (s32[64,3]{0,1:T(4,128)S(1)}, s32[64,3]{0,1:T(4,128)}, u32[]{:S(2)}) copy-start(s32[64,3]{0,1:T(4,128)} %param.15) | copy-start | bytes 2308
  3.8 23.5 %collective-permute-start.1 = (f32[3,32,32,1]{2,1,3,0:T(8,128)S(1)}, f32[3,32,32,1]{2,1,3,0:T(8,128)S(1)}, u32[]{:S(2)}, u32[]{:S(2)}) collective-permute-start(f32[3,32,32,1]{2,1,3,0:T(8,128)S(1)} %copy.121), channel_id=1, source_target_pairs={{1,0},{3,2},{5,4},{7,6},{9,8},{11,10},{13,12},{15,14},{17,16},{19,... | collective-permute-start | bytes 36872 | tf_op jit(solution)/shard_map/ppermute | solution.py:263
  5.7 21.7 %collective-permute-start = (f32[3,32,32,1]{2,1,3,0:T(8,128)S(1)}, f32[3,32,32,1]{2,1,3,0:T(8,128)S(1)}, u32[]{:S(2)}, u32[]{:S(2)}) collective-permute-start(f32[3,32,32,1]{2,1,3,0:T(8,128)S(1)} %copy.120), channel_id=1, source_target_pairs={{0,1},{2,3},{4,5},{6,7},{8,9},{10,11},{12,13},{14,15},{16,17},{18,... | collective-permute-start | bytes 36872 | tf_op jit(solution)/shard_map/ppermute | solution.py:262
  27.6 8.2 %collective-permute-start.2 = (f32[3,1,32,258]{3,2,1,0:T(8,128)S(1)}, f32[3,1,32,258]{3,2,1,0:T(8,128)S(1)}, u32[]{:S(2)}, u32[]{:S(2)}) collective-permute-start(f32[3,1,32,258]{3,2,1,0:T(8,128)S(1)} %pad_maximum_fusion.3), channel_id=1, source_target_pairs={{0,8},{8,16},{16,24},{1,9},{9,17},{17,25},{2,10},{10,18},{18,26},{... | collective-permute-start | bytes 297224 | tf_op jit(solution)/shard_map/ppermute | solution.py:262
  32.9 7.0 %collective-permute-start.3 = (f32[3,1,32,258]{3,2,1,0:T(8,128)S(1)}, f32[3,1,32,258]{3,2,1,0:T(8,128)S(1)}, u32[]{:S(2)}, u32[]{:S(2)}) collective-permute-start(f32[3,1,32,258]{3,2,1,0:T(8,128)S(1)} %pad_maximum_fusion.4), channel_id=1, source_target_pairs={{8,0},{16,8},{24,16},{9,1},{17,9},{25,17},{10,2},{18,10},{26,18},{... | collective-permute-start | bytes 297224 | tf_op jit(solution)/shard_map/ppermute | solution.py:263
  40.1 8.3 %collective-permute-start.5 = (f32[3,34,1,258]{3,1,2,0:T(8,128)S(1)}, f32[3,34,1,258]{3,1,2,0:T(8,128)S(1)}, u32[]{:S(2)}, u32[]{:S(2)}) collective-permute-start(f32[3,34,1,258]{3,1,2,0:T(8,128)S(1)} %pad_maximum_fusion.2), channel_id=1, source_target_pairs={{2,0},{4,2},{6,4},{3,1},{5,3},{7,5},{10,8},{12,10},{14,12},{11,9},... | collective-permute-start | bytes 315800 | tf_op jit(solution)/shard_map/ppermute | solution.py:263
  41.5 7.6 %collective-permute-start.4 = (f32[3,34,1,258]{3,1,2,0:T(8,128)S(1)}, f32[3,34,1,258]{3,1,2,0:T(8,128)S(1)}, u32[]{:S(2)}, u32[]{:S(2)}) collective-permute-start(f32[3,34,1,258]{3,1,2,0:T(8,128)S(1)} %pad_maximum_fusion.1), channel_id=1, source_target_pairs={{0,2},{2,4},{4,6},{1,3},{3,5},{5,7},{8,10},{10,12},{12,14},{9,11},... | collective-permute-start | bytes 315800 | tf_op jit(solution)/shard_map/ppermute | solution.py:262
  84.2 6.7 %copy-start = (f32[3,4,16,256]{3,2,1,0:T(8,128)S(1)}, f32[3,4,16,256]{3,2,1,0:T(8,128)}, u32[]{:S(2)}) copy-start(f32[3,4,16,256]{3,2,1,0:T(8,128)} %get-tuple-element.83) | copy-start | bytes 589828

commit v3 on v2

--- a/solution.py
+++ b/solution.py
@@ -238,6 +238,90 @@
         picked[s] = value
 
 
+def plan_kernel(ny, nz, bricks, corners, grid_slot, neighbors, flags, at, chosen, held):
+    ix, iy, iz = lax.axis_index("gx"), lax.axis_index("gy"), lax.axis_index("gz")
+    device = (ix * ny + iy) * nz + iz
+    total = held.shape[0]
+
+    def put(group, s, value):
+        flags[1 + group * SLOTS + s] = value
+
+    def clear(i, c):
+        for j in range(8):
+            held[i * 8 + j] = -1
+        return c
+
+    lax.fori_loop(0, total // 8, clear, 0)
+    for s in range(SLOTS):
+        put(12, s, 0)
+        put(13, s, 0)
+        chosen[s] = 0
+    for i in range(3):
+        at[i] = 0
+
+    def scan(g, c):
+        held[grid_slot[g]] = g
+        x, y, z = corners[0, g], corners[1, g], corners[2, g]
+        mine = (x // bricks[0] == ix) & (y // bricks[1] == iy) & (z // bricks[2] == iz)
+
+        @pl.when(mine)
+        def _():
+            box = lax.rem(x, bricks[0]) // B
+            flags[1 + 12 * SLOTS + box] = grid_slot[g] // (SLOTS * nz)
+            flags[1 + 13 * SLOTS + box] = lax.rem(grid_slot[g], SLOTS)
+            at[0] = lax.rem(y, bricks[1])
+            at[1] = lax.rem(z, bricks[2])
+            at[2] = 1
+
+        return c
+
+    lax.fori_loop(0, grid_slot.shape[0], scan, 0)
+
+    def leaves(n, side):
+        grid = held[n]
+        near = neighbors[1 - side, jnp.maximum(grid, 0)]
+        other = grid_slot[jnp.maximum(near, 0)] // SLOTS
+        return jnp.where((grid >= 0) & (near >= 0) & (other != n // SLOTS), 1, 0)
+
+    def rank_of(n, side):
+        first = n // SLOTS * SLOTS
+        rank = 0 if side == 0 else leaves(n, 0)
+        for s in range(SLOTS):
+            both = leaves(first + s, 0) + leaves(first + s, 1)
+            rank = rank + jnp.where(first + s < n, both, 0)
+        return rank
+
+    home = jnp.int32(0)
+    count = jnp.int32(0)
+    for s in range(SLOTS):
+        n = device * SLOTS + s
+        grid = held[n]
+        active = grid >= 0
+        g = jnp.maximum(grid, 0)
+        put(0, s, jnp.where(active, 1, 0))
+        put(1, s, jnp.where(active, lax.rem(corners[0, g], bricks[0]) // B, 0))
+        here = corners[0, g] // bricks[0] * ny + corners[1, g] // bricks[1]
+        home = jnp.where(active, here, home)
+        for side in range(2):
+            base = 2 + 5 * side
+            near = neighbors[side, g]
+            m = grid_slot[jnp.maximum(near, 0)]
+            put(base, s, m // (SLOTS * nz))
+            put(base + 1, s, rank_of(m, side))
+            put(base + 2, s, lax.rem(m, SLOTS))
+            put(base + 3, s, jnp.where(m // SLOTS == device, 1, 0))
+            put(base + 4, s, jnp.where(active & (near >= 0), 1, 0))
+        for side in range(2):
+            out = leaves(n, side)
+
+            @pl.when(out > 0)
+            def _():
+                chosen[count] = s * 2 + side
+
+            count = count + out
+    flags[0] = home
+
+
 def coarse_kernel(at, field, rows, out):
     n = field.shape[0]
     out[...] = field[...]
@@ -266,7 +350,12 @@
 
 def cut_slab(field, y, z):
     nx, ny, nz = field.shape[1:]
-    zlo, zhi = shift(field[..., :1], field[..., -1:], "gz")
+    if lax.axis_size("gz") == 2:
+        upper = lax.axis_index("gz") == 1
+        other = lax.ppermute(jnp.where(upper, field[..., :1], field[..., -1:]), "gz", [(0, 1), (1, 0)])
+        zlo, zhi = jnp.where(upper, other, 0.0), jnp.where(upper, 0.0, other)
+    else:
+        zlo, zhi = shift(field[..., :1], field[..., -1:], "gz")
 
     def wide(part, lo, hi):
         return jnp.concatenate([lo, part, hi], axis=3)
@@ -299,71 +388,26 @@
     count_y = lax.axis_size("gy")
     count_z = lax.axis_size("gz")
     count = count_x * count_y
-    index_x = lax.axis_index("gx")
-    index_y = lax.axis_index("gy")
-    index_z = lax.axis_index("gz")
     brick_x, brick_y, brick_z = coarse_field.shape[1:]
-    my_device = (index_x * count_y + index_y) * count_z + index_z
-    slot_range = jnp.arange(SLOTS, dtype=jnp.int32)
-    home_x = corners[:, 0] // brick_x
-    home_y = corners[:, 1] // brick_y
-    home_z = corners[:, 2] // brick_z
-    in_brick = (home_x == index_x) & (home_y == index_y) & (home_z == index_z)
-    box_x = (corners[:, 0] - home_x * brick_x) // B
-    owner_group = grid_slot // (SLOTS * count_z)
-    owner_slot = grid_slot % SLOTS
-    owner_dev = grid_slot // SLOTS
-    grid_ids = jnp.arange(corners.shape[0], dtype=jnp.int32)
-
-    def pick(match, values):
-        return jnp.sum(jnp.where(match, values[None, :], 0), axis=1)
-
-    present = jnp.any(in_brick)
-    anchor_y = jnp.max(jnp.where(in_brick, corners[:, 1] - index_y * brick_y, 0))
-    anchor_z = jnp.max(jnp.where(in_brick, corners[:, 2] - index_z * brick_z, 0))
-    row_match = in_brick[None, :] & (box_x[None, :] == slot_range[:, None])
-    need_mean = pick(row_match, grid_slot)
-    own_match = grid_slot[None, :] == (my_device * SLOTS + slot_range)[:, None]
-    active = jnp.any(own_match, axis=1)
-    slot_box = pick(own_match, box_x)
-    home = jnp.max(jnp.where(own_match, (home_x * count_y + home_y)[None, :], 0))
-    near_low = pick(own_match, neighbors[:, 0])
-    near_high = pick(own_match, neighbors[:, 1])
-
-    leaves = []
-    for side in range(2):
-        near_all = neighbors[:, 1 - side]
-        near_dev = pick(grid_ids[None, :] == near_all[:, None], owner_dev)
-        leaves.append((near_all >= 0) & (near_dev != owner_dev))
-    same = owner_dev[None, :] == owner_dev[:, None]
-    ahead = same & (owner_slot[None, :] < owner_slot[:, None])
-    before = pick(ahead, leaves[0].astype(jnp.int32) + leaves[1].astype(jnp.int32))
-    ranks = (before, before + leaves[0].astype(jnp.int32))
-    own = owner_dev == my_device
-    plane_range = jnp.arange(PLANES, dtype=jnp.int32)
-    chosen = jnp.zeros((PLANES,), jnp.int32)
-    for side in range(2):
-        match = (own & leaves[side])[None, :] & (ranks[side][None, :] == plane_range[:, None])
-        chosen = chosen + pick(match, owner_slot * 2 + side)
-    parts = [home[None], active.astype(jnp.int32), slot_box]
-    for side, near in ((0, near_low), (1, near_high)):
-        match = grid_ids[None, :] == near[:, None]
-        local = pick(match, owner_dev) == my_device
-        parts += [
-            pick(match, owner_group),
-            pick(match, ranks[side]),
-            pick(match, owner_slot),
-            local.astype(jnp.int32),
-            (active & (near >= 0)).astype(jnp.int32),
-        ]
-    parts += [need_mean // (SLOTS * count_z), need_mean % SLOTS]
-    flags = jnp.concatenate(parts).astype(jnp.int32)
+    smem = pl.BlockSpec(memory_space=pltpu.SMEM)
+    flags, at, chosen = pl.pallas_call(
+        functools.partial(plan_kernel, count_y, count_z, (brick_x, brick_y, brick_z)),
+        out_shape=(
+            jax.ShapeDtypeStruct((1 + 14 * SLOTS,), jnp.int32),
+            jax.ShapeDtypeStruct((3,), jnp.int32),
+            jax.ShapeDtypeStruct((PLANES,), jnp.int32),
+        ),
+        in_specs=[smem] * 3,
+        out_specs=(smem, smem, smem),
+        scratch_shapes=[pltpu.SMEM((count * count_z * SLOTS,), jnp.int32)],
+        name="plan",
+    )(corners.T, grid_slot, neighbors.T)
+    anchor_y, anchor_z = at[0], at[1]
 
     slab = cut_slab(coarse_field, anchor_y, anchor_z)
     columns, lines, places, across = edge_matrices(brick_x + 2)
     edge_rows = lines.shape[1]
     vmem = pl.BlockSpec(memory_space=pltpu.VMEM)
-    smem = pl.BlockSpec(memory_space=pltpu.SMEM)
     edges, planes = pl.pallas_call(
         edge_kernel,
         out_shape=(
@@ -402,7 +446,6 @@
     )
     rows = picked[:, : 3 * (B // 2)].reshape(SLOTS, 3, B // 2, 2, B * B)
     rows = rows.transpose(1, 0, 3, 2, 4).reshape(3 * brick_x, B * B)
-    at = jnp.stack([anchor_y, anchor_z, present.astype(jnp.int32)]).astype(jnp.int32)
     block = 16
     coarse_out = pl.pallas_call(
         coarse_kernel,

time: 92.3 us -> 92 us (level)
  Pallas kernels: 38.9 us -> 47.6 us
  other arithmetic: 6.91 us -> 1.52 us
  starting transfers between devices: 16.4 us -> 12.2 us
  waiting for transfers between devices: 6.32 us -> 7.98 us
    pallas_call x0 -> x1, Pallas kernels: none -> 4.74 us  [on_device(): pl.pallas_call(functools.partial(plan_kernel, count_y, count_z, (brick_x,...]
    pallas_call x1, Pallas kernels: 29.5 us -> 33.5 us  [on_device(): pl.pallas_call(functools.partial(fine_kernel, count_x, count_y, brick_x +...]
    ppermute x3 -> x2, starting transfers between devices: 12.6 us -> 9.05 us  [shift(): low = lax.ppermute(high_part, axis, [(i, i + 1) for i in range(count - 1)])]
    another operation x1 -> x0, other arithmetic: 1.83 us -> none  [on_device(): jnp.stack([anchor_y, anchor_z, present.astype(jnp.int32)]).astype(jnp.int32)]
    reduce_sum x4 -> x0, other arithmetic: 1.53 us -> none  [pick(): return jnp.sum(jnp.where(match, values[None, :], 0), axis=1)]
    ppermute x3 -> x2, waiting for transfers between devices: 0.55 us -> 2.02 us  [shift(): low = lax.ppermute(high_part, axis, [(i, i + 1) for i in range(count - 1)])]
    concatenate x1 -> x0, local copies, waits for them, and re-layouts: 1.35 us -> none  [on_device(): flags = jnp.concatenate(parts).astype(jnp.int32)]
    slice x1 -> x2, local copies, waits for them, and re-layouts: 2.46 us -> 3.79 us  [the longest x1 2.46 us: cut_slab(): field[..., -1:]]
  transfers between devices with their start and end apart: 6 -> 5, of which waited for: 3 -> 4; matrix products, arithmetic and copies ran while one was open for 16% -> 9% of each run, Pallas kernels for 0% -> 5%
where the time goes in v3:
time: 92 us; the launch traced here: 91.4 us
  Pallas kernels  47.6 us (52%)
  local copies, waits for them, and re-layouts  14.7 us (16%)
  starting transfers between devices  12.2 us (13%)
  waiting for transfers between devices  7.98 us (9%)
  between operations  7.38 us (8%)
  other arithmetic  1.52 us (2%)
    pallas_call x1, Pallas kernels, on_device(): pl.pallas_call(functools.partial(fine_kernel, count_x, count_y, brick_x +...  33.5 us
    ppermute x2, starting transfers between devices, shift(): low = lax.ppermute(high_part, axis, [(i, i + 1) for i in range(count - 1)])  9.05 us
    pallas_call x1, Pallas kernels, on_device(): pl.pallas_call(coarse_kernel, out_shape=jax.ShapeDtypeStruct((3 * brick_x...  6.68 us
    ppermute x2, waiting for transfers between devices, shift(): high = lax.ppermute(low_part, axis, [(i + 1, i) for i in range(count - 1)])  5.95 us
    dynamic_slice x10, local copies, waits for them, and re-layouts, cut(): return lax.dynamic_slice_in_dim(a, start, size, axis=2)  5.06 us
    pallas_call x1, Pallas kernels, on_device(): pl.pallas_call(functools.partial(plan_kernel, count_y, count_z, (brick_x,...  4.74 us
    pallas_call x1, Pallas kernels, on_device(): pl.pallas_call(edge_kernel, out_shape=(jax.ShapeDtypeStruct((edge_rows, L...  2.65 us
    ppermute x2, starting transfers between devices, shift(): high = lax.ppermute(low_part, axis, [(i + 1, i) for i in range(count - 1)])  2.58 us
  transfers between devices with their start and end apart: 5, of which 4 were waited for; matrix products, arithmetic and copies ran while one was open for 9% of the time, Pallas kernels for 5%

profile of v3, /device:TPU:0, one launch (start us, length us, event | category | flops | bytes accessed | tf_op | source)
XLA Modules:
  0.0 91.4 jit_solution(15147498213976589490)
XLA Ops:
  0.6 2.5 %fusion.20 = (f32[3,32,32,1]{3,2,1,0:T(8,128)S(1)}, f32[3,32,32,1]{3,2,1,0:T(8,128)S(1)}) fusion(f32[3,32,32,256]{3,2,1,0:T(8,128)} %param.12), kind=kLoop, calls=%fused_computation.66 | loop fusion | bytes 49152 | tf_op jit(solution)/shard_map/slice | solution.py:355
  3.1 0.6 copy.120
  3.7 0.6 copy.121
  4.4 0.6 collective-permute-start
  4.9 1.0 %fusion.19 = (f32[3,1,32,256]{3,2,1,0:T(8,128)S(1)}, f32[3,1,32,256]{3,2,1,0:T(8,128)S(1)}) fusion(f32[3,32,32,256]{3,2,1,0:T(8,128)} %param.12), kind=kLoop, calls=%fused_computation.65 | loop fusion | bytes 393216 | tf_op jit(solution)/shard_map/slice | solution.py:363
  5.9 4.7 %plan.1 = (s32[57]{0:T(128)}, s32[3]{0:T(128)}, s32[4]{0:T(128)}) custom-call(s32[3,64]{1,0:T(4,128)} %bitcast.46, s32[64]{0:T(128)} %grid_slot.1, s32[2,64]{1,0:T(2,128)} %bitcast.47), custom_call_target="tpu_custom_call" | custom-call | tf_op jit(solution)/shard_map/plan/pallas_call | solution.py:393
  10.6 1.3 %fusion.23 = (s32[1]{0:T(128)}, s32[1]{0:T(128)}) fusion(s32[3]{0:T(128)} %get-tuple-element.11.at), kind=kLoop, calls=%fused_computation.69 | loop fusion | bytes 16 | tf_op jit(solution)/shard_map/slice | solution.py:405
  14.6 2.2 %fusion.18 = (f32[3,32,1,256]{3,2,1,0:T(1,128)S(1)}, f32[3,32,1,256]{3,2,1,0:T(1,128)S(1)}, f32[3,32,1,256]{3,2,1,0:T(1,128)S(1)}, f32[3,32,1,256]{3,2,1,0:T(1,128)S(1)}) fusion(f32[3,32,32,256]{3,2,1,0:T(8,128)} %param.12, s32[]{:T(128)S(6)} %max.3, s32[]{:T(128)S(6)} %select_n.69), kind=kLoop, calls=%fused_computation.64 | loop fusion | bytes 786440 | tf_op jit(solution)/shard_map/dynamic_slice | solution.py:369
  17.5 1.3 %constant_dynamic-slice_fusion.4 = f32[3,32,8,256]{3,2,1,0:T(8,128)S(1)} fusion(f32[3,32,32,256]{3,2,1,0:T(8,128)} %param.12, s32[]{:T(128)S(6)} %select_n.67), kind=kLoop, calls=%fused_computation.49 | loop fusion | bytes 1572868 | tf_op jit(solution)/shard_map/dynamic_slice | solution.py:369
  22.0 0.0 collective-permute-done
  22.1 0.1 slice_bitcast_fusion.2
  22.2 0.1 copy.88
  22.3 0.1 copy.87
  22.4 0.1 pad_maximum_fusion.3
  22.6 4.5 %collective-permute-start.1 = (f32[3,1,32,258]{3,2,1,0:T(8,128)S(1)}, f32[3,1,32,258]{3,2,1,0:T(8,128)S(1)}, u32[]{:S(2)}, u32[]{:S(2)}) collective-permute-start(f32[3,1,32,258]{3,2,1,0:T(8,128)S(1)} %pad_maximum_fusion.3), channel_id=1, source_target_pairs={{0,8},{8,16},{16,24},{1,9},{9,17},{17,25},{2,10},{10,18},{18,26},{... | collective-permute-start | bytes 297224 | tf_op jit(solution)/shard_map/ppermute | solution.py:346
  27.1 0.1 copy.93
  27.2 0.1 copy.92
  27.3 0.1 pad_maximum_fusion.4
  27.4 1.3 %collective-permute-start.2 = (f32[3,1,32,258]{3,2,1,0:T(8,128)S(1)}, f32[3,1,32,258]{3,2,1,0:T(8,128)S(1)}, u32[]{:S(2)}, u32[]{:S(2)}) collective-permute-start(f32[3,1,32,258]{3,2,1,0:T(8,128)S(1)} %pad_maximum_fusion.4), channel_id=1, source_target_pairs={{8,0},{16,8},{24,16},{9,1},{17,9},{25,17},{10,2},{18,10},{26,18},{... | collective-permute-start | bytes 297224 | tf_op jit(solution)/shard_map/ppermute | solution.py:347
  28.7 0.1 constant_dynamic-slice_fusion.3
  28.8 0.6 copy.101
  29.4 0.6 copy.102
  30.0 1.0 %collective-permute-done.1 = f32[3,1,32,258]{3,2,1,0:T(8,128)S(1)} collective-permute-done((f32[3,1,32,258]{3,2,1,0:T(8,128)S(1)}, f32[3,1,32,258]{3,2,1,0:T(8,128)S(1)}, u32[]{:S(2)}, u32[]{:S(2)}) %collective-permute-start.1) | collective-permute-done | bytes 99104 | tf_op jit(solution)/shard_map/ppermute | solution.py:346
  31.1 4.4 %collective-permute-done.2 = f32[3,1,32,258]{3,2,1,0:T(8,128)S(1)} collective-permute-done((f32[3,1,32,258]{3,2,1,0:T(8,128)S(1)}, f32[3,1,32,258]{3,2,1,0:T(8,128)S(1)}, u32[]{:S(2)}, u32[]{:S(2)}) %collective-permute-start.2) | collective-permute-done | bytes 99104 | tf_op jit(solution)/shard_map/ppermute | solution.py:347
  35.5 0.1 pad_maximum_fusion.2
  35.6 1.3 %collective-permute-start.4 = (f32[3,34,1,258]{3,1,2,0:T(8,128)S(1)}, f32[3,34,1,258]{3,1,2,0:T(8,128)S(1)}, u32[]{:S(2)}, u32[]{:S(2)}) collective-permute-start(f32[3,34,1,258]{3,1,2,0:T(8,128)S(1)} %pad_maximum_fusion.2), channel_id=1, source_target_pairs={{2,0},{4,2},{6,4},{3,1},{5,3},{7,5},{10,8},{12,10},{14,12},{11,9},... | collective-permute-start | bytes 315800 | tf_op jit(solution)/shard_map/ppermute | solution.py:347
  36.9 0.1 pad_maximum_fusion.1
  37.1 4.6 %collective-permute-start.3 = (f32[3,34,1,258]{3,1,2,0:T(8,128)S(1)}, f32[3,34,1,258]{3,1,2,0:T(8,128)S(1)}, u32[]{:S(2)}, u32[]{:S(2)}) collective-permute-start(f32[3,34,1,258]{3,1,2,0:T(8,128)S(1)} %pad_maximum_fusion.1), channel_id=1, source_target_pairs={{0,2},{2,4},{4,6},{1,3},{3,5},{5,7},{8,10},{10,12},{12,14},{9,11},... | collective-permute-start | bytes 315800 | tf_op jit(solution)/shard_map/ppermute | solution.py:346
  41.7 0.5 fusion.1
  42.2 1.5 %collective-permute-done.4 = f32[3,34,1,258]{3,1,2,0:T(8,128)S(1)} collective-permute-done((f32[3,34,1,258]{3,1,2,0:T(8,128)S(1)}, f32[3,34,1,258]{3,1,2,0:T(8,128)S(1)}, u32[]{:S(2)}, u32[]{:S(2)}) %collective-permute-start.4) | collective-permute-done | bytes 105296 | tf_op jit(solution)/shard_map/ppermute | solution.py:347
  43.7 0.2 fusion.6
  43.9 0.1 copy.114
  44.0 1.0 %collective-permute-done.3 = f32[3,34,1,258]{3,1,2,0:T(8,128)S(1)} collective-permute-done((f32[3,34,1,258]{3,1,2,0:T(8,128)S(1)}, f32[3,34,1,258]{3,1,2,0:T(8,128)S(1)}, u32[]{:S(2)}, u32[]{:S(2)}) %collective-permute-start.3) | collective-permute-done | bytes 105296 | tf_op jit(solution)/shard_map/ppermute | solution.py:346
  45.0 0.2 fusion.11
  45.1 0.1 copy.113
  45.2 0.2 pad_maximum_fusion
  45.4 0.3 reshape.24
  45.7 0.6 pad.4.slab
  46.3 2.7 %edge_cut.1 = (f32[40,128]{1,0:T(8,128)}, f32[24,128]{1,0:T(8,128)}) custom-call(s32[4]{0:T(128)} %get-tuple-element.10.chosen, f32[104,128]{1,0:T(8,128)} %pad.4.slab, f32[3,4,16,256]{3,2,1,0:T(8,128)} %fine.3, f32[3,128,128]{2,1,0:T(8,128)} %constant.36.clone.columns, f32[4,40,104]{2,1,0:T(8,128)} %constant.37.clone.lines), custom_call_target="tpu_custom_call" | custom-call | tf_op jit(solution)/shard_map/edge_cut/pallas_call | solution.py:411
  49.0 33.5 %fine_step.1 = (f32[3,4,16,256]{3,2,1,0:T(8,128)}, f32[4,12,128]{2,1,0:T(8,128)}) custom-call(s32[57]{0:T(128)} %get-tuple-element.9.flags, f32[40,128]{1,0:T(8,128)} %get-tuple-element.12.edges, f32[24,128]{1,0:T(8,128)} %get-tuple-element.13.planes, f32[3,4,16,256]{3,2,1,0:T(8,128)} %fine.3, f32[4,16,256]{2,1,0:T(8,128)} %visc.1, ...), custom_call_target="tpu_custom_call" | custom-call | tf_op jit(solution)/shard_map/fine_step/pallas_call | solution.py:423
  82.5 0.8 copy.117
  83.3 0.1 reshape.21
  83.4 0.6 copy.118
  84.0 0.0 copy-start
  84.0 6.7 %coarse_fill.1 = f32[96,32,256]{2,1,0:T(8,128)} custom-call(s32[3]{0:T(128)} %get-tuple-element.11.at, f32[96,32,256]{2,1,0:T(8,128)} %bitcast.42, f32[96,64]{1,0:T(8,128)} %bitcast.44), custom_call_target="tpu_custom_call" | custom-call | tf_op jit(solution)/shard_map/coarse_fill/pallas_call | solution.py:450
  90.7 0.0 copy-done
  90.7 0.7 copy.127
  (11 shorter events, 0.1 us)
Async XLA Ops:
  4.4 17.7 %collective-permute-start = (f32[3,32,32,1]{2,1,3,0:T(8,128)S(1)}, f32[3,32,32,1]{2,1,3,0:T(8,128)S(1)}, u32[]{:S(2)}, u32[]{:S(2)}) collective-permute-start(f32[3,32,32,1]{2,1,3,0:T(8,128)S(1)} %broadcast_select_fusion.2), channel_id=1, source_target_pairs={{0,1},{1,0},{2,3},{3,2},{4,5},{5,4},{6,7},{7,6},{8,9},{9,8},{10,11... | collective-permute-start | bytes 36872 | tf_op jit(solution)/shard_map/ppermute | solution.py:355
  22.6 8.5 %collective-permute-start.1 = (f32[3,1,32,258]{3,2,1,0:T(8,128)S(1)}, f32[3,1,32,258]{3,2,1,0:T(8,128)S(1)}, u32[]{:S(2)}, u32[]{:S(2)}) collective-permute-start(f32[3,1,32,258]{3,2,1,0:T(8,128)S(1)} %pad_maximum_fusion.3), channel_id=1, source_target_pairs={{0,8},{8,16},{16,24},{1,9},{9,17},{17,25},{2,10},{10,18},{18,26},{... | collective-permute-start | bytes 297224 | tf_op jit(solution)/shard_map/ppermute | solution.py:346
  27.4 8.1 %collective-permute-start.2 = (f32[3,1,32,258]{3,2,1,0:T(8,128)S(1)}, f32[3,1,32,258]{3,2,1,0:T(8,128)S(1)}, u32[]{:S(2)}, u32[]{:S(2)}) collective-permute-start(f32[3,1,32,258]{3,2,1,0:T(8,128)S(1)} %pad_maximum_fusion.4), channel_id=1, source_target_pairs={{8,0},{16,8},{24,16},{9,1},{17,9},{25,17},{10,2},{18,10},{26,18},{... | collective-permute-start | bytes 297224 | tf_op jit(solution)/shard_map/ppermute | solution.py:347
  35.6 8.1 %collective-permute-start.4 = (f32[3,34,1,258]{3,1,2,0:T(8,128)S(1)}, f32[3,34,1,258]{3,1,2,0:T(8,128)S(1)}, u32[]{:S(2)}, u32[]{:S(2)}) collective-permute-start(f32[3,34,1,258]{3,1,2,0:T(8,128)S(1)} %pad_maximum_fusion.2), channel_id=1, source_target_pairs={{2,0},{4,2},{6,4},{3,1},{5,3},{7,5},{10,8},{12,10},{14,12},{11,9},... | collective-permute-start | bytes 315800 | tf_op jit(solution)/shard_map/ppermute | solution.py:347
  37.1 7.9 %collective-permute-start.3 = (f32[3,34,1,258]{3,1,2,0:T(8,128)S(1)}, f32[3,34,1,258]{3,1,2,0:T(8,128)S(1)}, u32[]{:S(2)}, u32[]{:S(2)}) collective-permute-start(f32[3,34,1,258]{3,1,2,0:T(8,128)S(1)} %pad_maximum_fusion.1), channel_id=1, source_target_pairs={{0,2},{2,4},{4,6},{1,3},{3,5},{5,7},{8,10},{10,12},{12,14},{9,11},... | collective-permute-start | bytes 315800 | tf_op jit(solution)/shard_map/ppermute | solution.py:346
  84.0 6.7 %copy-start = (f32[3,4,16,256]{3,2,1,0:T(8,128)S(1)}, f32[3,4,16,256]{3,2,1,0:T(8,128)}, u32[]{:S(2)}) copy-start(f32[3,4,16,256]{3,2,1,0:T(8,128)} %get-tuple-element.58) | copy-start | bytes 589828

commit v4 on v3

--- a/solution.py
+++ b/solution.py
@@ -141,21 +141,28 @@
     own_plane.start()
     pl.semaphore_wait(barrier, count - 1)
 
-    def send(o, c):
+    def send_slab(o, c):
         slab_copy(o).start()
+        return c
+
+    def send_plane(o, c):
         plane_copy(o).start()
         return c
 
-    lax.fori_loop(1, count, send, 0)
+    lax.fori_loop(1, count, send_slab, 0)
+    lax.fori_loop(1, count, send_plane, 0)
     own_slab.wait()
     own_plane.wait()
 
-    def finish(o, c):
+    def finish_slab(o, c):
         slab_copy(o).wait()
+        return c
+
+    def finish_plane(o, c):
         plane_copy(o).wait()
         return c
 
-    lax.fori_loop(1, count, finish, 0)
+    lax.fori_loop(1, count, finish_slab, 0)
 
     def flag(group, s):
         return flags[1 + group * SLOTS + s]
@@ -174,6 +181,7 @@
     along = dot(blend, mine)
     ghosts = [dot(along, places[k]) for k in range(3)]
     xface = dot(mine, across[...])[width : width + 6]
+    lax.fori_loop(1, count, finish_plane, 0)
     lane = lax.broadcasted_iota(jnp.int32, (F, F * F), 1)
     row = lax.broadcasted_iota(jnp.int32, (F, F * F), 0)
     lz = lane % F

time: 92 us -> 87.9 us (0.955)
  Pallas kernels: 47.6 us -> 43.4 us
    pallas_call x1, Pallas kernels: 33.5 us -> 29.4 us  [on_device(): pl.pallas_call(functools.partial(fine_kernel, count_x, count_y, brick_x +...]
  transfers between devices with their start and end apart: 5 -> 5, of which waited for: 4 -> 4; matrix products, arithmetic and copies ran while one was open for 9% -> 10% of each run, Pallas kernels for 5% -> 5%
where the time goes in v4:
time: 87.9 us; the launch traced here: 87 us
  Pallas kernels  43.4 us (49%)
  local copies, waits for them, and re-layouts  14.9 us (17%)
  starting transfers between devices  12.2 us (14%)
  waiting for transfers between devices  7.58 us (9%)
  between operations  7.38 us (8%)
  other arithmetic  1.52 us (2%)
    pallas_call x1, Pallas kernels, on_device(): pl.pallas_call(functools.partial(fine_kernel, count_x, count_y, brick_x +...  29.4 us
    ppermute x2, starting transfers between devices, shift(): low = lax.ppermute(high_part, axis, [(i, i + 1) for i in range(count - 1)])  9.05 us
    pallas_call x1, Pallas kernels, on_device(): pl.pallas_call(coarse_kernel, out_shape=jax.ShapeDtypeStruct((3 * brick_x...  6.67 us
    ppermute x2, waiting for transfers between devices, shift(): high = lax.ppermute(low_part, axis, [(i + 1, i) for i in range(count - 1)])  5.92 us
    dynamic_slice x10, local copies, waits for them, and re-layouts, cut(): return lax.dynamic_slice_in_dim(a, start, size, axis=2)  5.26 us
    pallas_call x1, Pallas kernels, on_device(): pl.pallas_call(functools.partial(plan_kernel, count_y, count_z, (brick_x,...  4.74 us
    pallas_call x1, Pallas kernels, on_device(): pl.pallas_call(edge_kernel, out_shape=(jax.ShapeDtypeStruct((edge_rows, L...  2.65 us
    ppermute x2, starting transfers between devices, shift(): high = lax.ppermute(low_part, axis, [(i + 1, i) for i in range(count - 1)])  2.58 us
  transfers between devices with their start and end apart: 5, of which 4 were waited for; matrix products, arithmetic and copies ran while one was open for 10% of the time, Pallas kernels for 5%

profile of v4, /device:TPU:0, one launch (start us, length us, event | category | flops | bytes accessed | tf_op | source)
XLA Modules:
  0.0 87.0 jit_solution(11695273669293670969)
XLA Ops:
  0.6 2.5 %fusion.20 = (f32[3,32,32,1]{3,2,1,0:T(8,128)S(1)}, f32[3,32,32,1]{3,2,1,0:T(8,128)S(1)}) fusion(f32[3,32,32,256]{3,2,1,0:T(8,128)} %param.12), kind=kLoop, calls=%fused_computation.66 | loop fusion | bytes 49152 | tf_op jit(solution)/shard_map/slice | solution.py:363
  3.1 0.6 copy.120
  3.7 0.6 copy.121
  4.4 0.6 collective-permute-start
  4.9 1.0 %fusion.19 = (f32[3,1,32,256]{3,2,1,0:T(8,128)S(1)}, f32[3,1,32,256]{3,2,1,0:T(8,128)S(1)}) fusion(f32[3,32,32,256]{3,2,1,0:T(8,128)} %param.12), kind=kLoop, calls=%fused_computation.65 | loop fusion | bytes 393216 | tf_op jit(solution)/shard_map/slice | solution.py:371
  5.9 4.7 %plan.1 = (s32[57]{0:T(128)}, s32[3]{0:T(128)}, s32[4]{0:T(128)}) custom-call(s32[3,64]{1,0:T(4,128)} %bitcast.46, s32[64]{0:T(128)} %grid_slot.1, s32[2,64]{1,0:T(2,128)} %bitcast.47), custom_call_target="tpu_custom_call" | custom-call | tf_op jit(solution)/shard_map/plan/pallas_call | solution.py:401
  10.6 1.3 %fusion.23 = (s32[1]{0:T(128)}, s32[1]{0:T(128)}) fusion(s32[3]{0:T(128)} %get-tuple-element.11.at), kind=kLoop, calls=%fused_computation.69 | loop fusion | bytes 16 | tf_op jit(solution)/shard_map/slice | solution.py:413
  14.6 2.2 %fusion.18 = (f32[3,32,1,256]{3,2,1,0:T(1,128)S(1)}, f32[3,32,1,256]{3,2,1,0:T(1,128)S(1)}, f32[3,32,1,256]{3,2,1,0:T(1,128)S(1)}, f32[3,32,1,256]{3,2,1,0:T(1,128)S(1)}) fusion(f32[3,32,32,256]{3,2,1,0:T(8,128)} %param.12, s32[]{:T(128)S(6)} %max.3, s32[]{:T(128)S(6)} %select_n.69), kind=kLoop, calls=%fused_computation.64 | loop fusion | bytes 786440 | tf_op jit(solution)/shard_map/dynamic_slice | solution.py:377
  17.4 1.5 %constant_dynamic-slice_fusion.4 = f32[3,32,8,256]{3,2,1,0:T(8,128)S(1)} fusion(f32[3,32,32,256]{3,2,1,0:T(8,128)} %param.12, s32[]{:T(128)S(6)} %select_n.67), kind=kLoop, calls=%fused_computation.49 | loop fusion | bytes 1572868 | tf_op jit(solution)/shard_map/dynamic_slice | solution.py:377
  22.2 0.0 collective-permute-done
  22.3 0.1 slice_bitcast_fusion.2
  22.4 0.1 copy.88
  22.5 0.1 copy.87
  22.6 0.1 pad_maximum_fusion.3
  22.8 4.5 %collective-permute-start.1 = (f32[3,1,32,258]{3,2,1,0:T(8,128)S(1)}, f32[3,1,32,258]{3,2,1,0:T(8,128)S(1)}, u32[]{:S(2)}, u32[]{:S(2)}) collective-permute-start(f32[3,1,32,258]{3,2,1,0:T(8,128)S(1)} %pad_maximum_fusion.3), channel_id=1, source_target_pairs={{0,8},{8,16},{16,24},{1,9},{9,17},{17,25},{2,10},{10,18},{18,26},{... | collective-permute-start | bytes 297224 | tf_op jit(solution)/shard_map/ppermute | solution.py:354
  27.3 0.1 copy.93
  27.4 0.1 copy.92
  27.5 0.1 pad_maximum_fusion.4
  27.6 1.3 %collective-permute-start.2 = (f32[3,1,32,258]{3,2,1,0:T(8,128)S(1)}, f32[3,1,32,258]{3,2,1,0:T(8,128)S(1)}, u32[]{:S(2)}, u32[]{:S(2)}) collective-permute-start(f32[3,1,32,258]{3,2,1,0:T(8,128)S(1)} %pad_maximum_fusion.4), channel_id=1, source_target_pairs={{8,0},{16,8},{24,16},{9,1},{17,9},{25,17},{10,2},{18,10},{26,18},{... | collective-permute-start | bytes 297224 | tf_op jit(solution)/shard_map/ppermute | solution.py:355
  28.9 0.1 constant_dynamic-slice_fusion.3
  29.0 0.6 copy.101
  29.6 0.6 copy.102
  30.2 0.8 collective-permute-done.1
  31.1 4.4 %collective-permute-done.2 = f32[3,1,32,258]{3,2,1,0:T(8,128)S(1)} collective-permute-done((f32[3,1,32,258]{3,2,1,0:T(8,128)S(1)}, f32[3,1,32,258]{3,2,1,0:T(8,128)S(1)}, u32[]{:S(2)}, u32[]{:S(2)}) %collective-permute-start.2) | collective-permute-done | bytes 99104 | tf_op jit(solution)/shard_map/ppermute | solution.py:355
  35.5 0.1 pad_maximum_fusion.2
  35.6 1.3 %collective-permute-start.4 = (f32[3,34,1,258]{3,1,2,0:T(8,128)S(1)}, f32[3,34,1,258]{3,1,2,0:T(8,128)S(1)}, u32[]{:S(2)}, u32[]{:S(2)}) collective-permute-start(f32[3,34,1,258]{3,1,2,0:T(8,128)S(1)} %pad_maximum_fusion.2), channel_id=1, source_target_pairs={{2,0},{4,2},{6,4},{3,1},{5,3},{7,5},{10,8},{12,10},{14,12},{11,9},... | collective-permute-start | bytes 315800 | tf_op jit(solution)/shard_map/ppermute | solution.py:355
  36.9 0.1 pad_maximum_fusion.1
  37.1 4.6 %collective-permute-start.3 = (f32[3,34,1,258]{3,1,2,0:T(8,128)S(1)}, f32[3,34,1,258]{3,1,2,0:T(8,128)S(1)}, u32[]{:S(2)}, u32[]{:S(2)}) collective-permute-start(f32[3,34,1,258]{3,1,2,0:T(8,128)S(1)} %pad_maximum_fusion.1), channel_id=1, source_target_pairs={{0,2},{2,4},{4,6},{1,3},{3,5},{5,7},{8,10},{10,12},{12,14},{9,11},... | collective-permute-start | bytes 315800 | tf_op jit(solution)/shard_map/ppermute | solution.py:354
  41.7 0.5 fusion.1
  42.2 1.5 %collective-permute-done.4 = f32[3,34,1,258]{3,1,2,0:T(8,128)S(1)} collective-permute-done((f32[3,34,1,258]{3,1,2,0:T(8,128)S(1)}, f32[3,34,1,258]{3,1,2,0:T(8,128)S(1)}, u32[]{:S(2)}, u32[]{:S(2)}) %collective-permute-start.4) | collective-permute-done | bytes 105296 | tf_op jit(solution)/shard_map/ppermute | solution.py:355
  43.7 0.2 fusion.6
  43.9 0.1 copy.114
  43.9 0.9 collective-permute-done.3
  44.8 0.2 fusion.11
  44.9 0.1 copy.113
  45.0 0.2 pad_maximum_fusion
  45.2 0.3 reshape.24
  45.5 0.6 pad.4.slab
  46.1 2.7 %edge_cut.1 = (f32[40,128]{1,0:T(8,128)}, f32[24,128]{1,0:T(8,128)}) custom-call(s32[4]{0:T(128)} %get-tuple-element.10.chosen, f32[104,128]{1,0:T(8,128)} %pad.4.slab, f32[3,4,16,256]{3,2,1,0:T(8,128)} %fine.3, f32[3,128,128]{2,1,0:T(8,128)} %constant.36.clone.columns, f32[4,40,104]{2,1,0:T(8,128)} %constant.37.clone.lines), custom_call_target="tpu_custom_call" | custom-call | tf_op jit(solution)/shard_map/edge_cut/pallas_call | solution.py:419
  48.8 29.4 %fine_step.1 = (f32[3,4,16,256]{3,2,1,0:T(8,128)}, f32[4,12,128]{2,1,0:T(8,128)}) custom-call(s32[57]{0:T(128)} %get-tuple-element.9.flags, f32[40,128]{1,0:T(8,128)} %get-tuple-element.12.edges, f32[24,128]{1,0:T(8,128)} %get-tuple-element.13.planes, f32[3,4,16,256]{3,2,1,0:T(8,128)} %fine.3, f32[4,16,256]{2,1,0:T(8,128)} %visc.1, ...), custom_call_target="tpu_custom_call" | custom-call | tf_op jit(solution)/shard_map/fine_step/pallas_call | solution.py:431
  78.1 0.8 copy.117
  78.9 0.1 reshape.21
  79.0 0.6 copy.118
  79.6 0.0 copy-start
  79.6 6.7 %coarse_fill.1 = f32[96,32,256]{2,1,0:T(8,128)} custom-call(s32[3]{0:T(128)} %get-tuple-element.11.at, f32[96,32,256]{2,1,0:T(8,128)} %bitcast.42, f32[96,64]{1,0:T(8,128)} %bitcast.44), custom_call_target="tpu_custom_call" | custom-call | tf_op jit(solution)/shard_map/coarse_fill/pallas_call | solution.py:458
  86.3 0.0 copy-done
  86.3 0.7 copy.127
  (11 shorter events, 0.1 us)
Async XLA Ops:
  4.4 17.9 %collective-permute-start = (f32[3,32,32,1]{2,1,3,0:T(8,128)S(1)}, f32[3,32,32,1]{2,1,3,0:T(8,128)S(1)}, u32[]{:S(2)}, u32[]{:S(2)}) collective-permute-start(f32[3,32,32,1]{2,1,3,0:T(8,128)S(1)} %broadcast_select_fusion.2), channel_id=1, source_target_pairs={{0,1},{1,0},{2,3},{3,2},{4,5},{5,4},{6,7},{7,6},{8,9},{9,8},{10,11... | collective-permute-start | bytes 36872 | tf_op jit(solution)/shard_map/ppermute | solution.py:363
  22.8 8.3 %collective-permute-start.1 = (f32[3,1,32,258]{3,2,1,0:T(8,128)S(1)}, f32[3,1,32,258]{3,2,1,0:T(8,128)S(1)}, u32[]{:S(2)}, u32[]{:S(2)}) collective-permute-start(f32[3,1,32,258]{3,2,1,0:T(8,128)S(1)} %pad_maximum_fusion.3), channel_id=1, source_target_pairs={{0,8},{8,16},{16,24},{1,9},{9,17},{17,25},{2,10},{10,18},{18,26},{... | collective-permute-start | bytes 297224 | tf_op jit(solution)/shard_map/ppermute | solution.py:354
  27.6 7.9 %collective-permute-start.2 = (f32[3,1,32,258]{3,2,1,0:T(8,128)S(1)}, f32[3,1,32,258]{3,2,1,0:T(8,128)S(1)}, u32[]{:S(2)}, u32[]{:S(2)}) collective-permute-start(f32[3,1,32,258]{3,2,1,0:T(8,128)S(1)} %pad_maximum_fusion.4), channel_id=1, source_target_pairs={{8,0},{16,8},{24,16},{9,1},{17,9},{25,17},{10,2},{18,10},{26,18},{... | collective-permute-start | bytes 297224 | tf_op jit(solution)/shard_map/ppermute | solution.py:355
  35.6 8.1 %collective-permute-start.4 = (f32[3,34,1,258]{3,1,2,0:T(8,128)S(1)}, f32[3,34,1,258]{3,1,2,0:T(8,128)S(1)}, u32[]{:S(2)}, u32[]{:S(2)}) collective-permute-start(f32[3,34,1,258]{3,1,2,0:T(8,128)S(1)} %pad_maximum_fusion.2), channel_id=1, source_target_pairs={{2,0},{4,2},{6,4},{3,1},{5,3},{7,5},{10,8},{12,10},{14,12},{11,9},... | collective-permute-start | bytes 315800 | tf_op jit(solution)/shard_map/ppermute | solution.py:355
  37.1 7.7 %collective-permute-start.3 = (f32[3,34,1,258]{3,1,2,0:T(8,128)S(1)}, f32[3,34,1,258]{3,1,2,0:T(8,128)S(1)}, u32[]{:S(2)}, u32[]{:S(2)}) collective-permute-start(f32[3,34,1,258]{3,1,2,0:T(8,128)S(1)} %pad_maximum_fusion.1), channel_id=1, source_target_pairs={{0,2},{2,4},{4,6},{1,3},{3,5},{5,7},{8,10},{10,12},{12,14},{9,11},... | collective-permute-start | bytes 315800 | tf_op jit(solution)/shard_map/ppermute | solution.py:354
  79.6 6.7 %copy-start = (f32[3,4,16,256]{3,2,1,0:T(8,128)S(1)}, f32[3,4,16,256]{3,2,1,0:T(8,128)}, u32[]{:S(2)}) copy-start(f32[3,4,16,256]{3,2,1,0:T(8,128)} %get-tuple-element.58) | copy-start | bytes 589828
